TPU v7x, 512 devices: a whole 4x8x8 slice. The times are simulated.
512 devices in a mesh: rep: 8 (over z_lo, core), blk: 64 (over z_hi, x, y).
Axes of the slice: x: 4, y: 8, z: 8 (z_hi: 2, z_lo: 4; z = z_hi * 4 + z_lo), core: 2. Of those that a mesh axis runs over, the one named last changes fastest.
Arguments:
- gradients: bfloat16 [8, 512, 8, 4096], P('rep', 'blk'), may hold values from -22 to 22
- left_stat: float32 [64, 512, 512], P('blk', 'rep'), as said below
- right_stat: float32 [64, 512, 512], P('blk', 'rep')
- momentum: float32 [64, 512, 512], P('blk', 'rep'), may hold values from -6 to 6
- master: float32 [64, 512, 512], P('blk', 'rep'), may hold values from -6 to 6
Outputs:
- params: bfloat16 [512, 8, 4096], P('blk')
- momentum_out: float32 [64, 512, 512], P('blk', 'rep')
- left_new: float32 [64, 512, 512], P('blk', 'rep')
- right_new: float32 [64, 512, 512], P('blk', 'rep')
Inputs may be any that keep to these rules, and one draw needn't show every extreme that they name: Every block of left_stat and right_stat is symmetric positive semidefinite.
All inputs are finite; a program needn't handle non-finite values.
Results may differ from a plain program's by a relative error of at most 0.005.
Values may be sent and summed in bfloat16 or wider, within the bound.
No kernel may reach another device: no remote copies, remote signals or barrier semaphores. Data moves between devices by JAX's collectives and lax.ppermute only.
A program may use at most 64 MiB of HBM per device.

v0:
```python
import jax
import jax.numpy as jnp
from jax import lax
from jax.sharding import Mesh
from jax.sharding import PartitionSpec as P

ITERS = 4
REP = ("rep_0", "rep_1")
BLK = ("blk_0", "blk_1", "blk_2")
REP_BLK = ("rep_0", "rep_1", "blk_0", "blk_1", "blk_2")


stat_decay = 0.9
moment_decay = 0.9
step_size = 0.25


def in_blocks(shard, dim, size):
    before, after = (shard.shape[:dim], shard.shape[dim + 1 :])
    return jnp.moveaxis(shard.reshape(*before, size, -1, *after), dim, 0)


def summed_on_arrival(shard, axis, dim):
    size = lax.axis_size(axis)
    pieces = lax.all_to_all(in_blocks(shard, dim, size), axis, 0, 0, tiled=True)
    return jnp.sum(pieces.astype(jnp.float32), axis=0)


def joined_along(pieces, dim):
    pieces = jnp.moveaxis(pieces, 0, dim)
    dims = pieces.shape
    return pieces.reshape(*dims[:dim], dims[dim] * dims[dim + 1], *dims[dim + 2 :])


def sent_to_all(shard, axis):
    copies = jnp.broadcast_to(shard, (lax.axis_size(axis), *shard.shape))
    return lax.all_to_all(copies, axis, split_axis=0, concat_axis=0, tiled=True)


def collect(shard, axis, dim):
    return joined_along(sent_to_all(shard, axis), dim)


def side_by_side(arrays, axis, dim, along):
    widths = [a.shape[along] for a in arrays]
    both = jnp.concatenate(arrays, axis=along)
    out = lax.all_gather(both, axis, axis=dim, tiled=True)
    return tuple(jnp.split(out, [sum(widths[:k]) for k in range(1, len(widths))], axis=along))


def side_by_side_2(arrays, axis, dim, along):
    widths = [a.shape[along] for a in arrays]
    both = jnp.concatenate(arrays, axis=along)
    out = collect(both, axis, dim)
    return tuple(jnp.split(out, [sum(widths[:k]) for k in range(1, len(widths))], axis=along))


def one_axis_at_a_time(shard, axes):
    for axis in axes:
        shard = lax.psum(shard, axis)
    return shard


def exact_dot(left, right):
    return jnp.dot(left, right, precision=lax.Precision.HIGHEST, preferred_element_type=jnp.float32)


def on_device(gradients, left_stat, right_stat, momentum, master):
    size_block = left_stat.shape[2]
    row_count = left_stat.shape[1]
    replicas = lax.axis_size(REP)
    owners = lax.axis_size(BLK)
    sub_rows = size_block // owners
    row_start = lax.axis_index(REP) * row_count
    flat_grad = gradients.reshape(sub_rows, owners * size_block)
    summed_rows = summed_on_arrival(
        flat_grad.astype(jnp.float32).reshape(sub_rows, owners, size_block).astype(jnp.bfloat16),
        REP,
        2,
    )
    moved_rows = lax.all_to_all(summed_rows, BLK, split_axis=1, concat_axis=0, tiled=True)
    summed = moved_rows.reshape(size_block, size_block // replicas)
    grad_cols = summed * (1.0 / replicas)
    grad_full = collect(grad_cols, REP, 1)
    right_gram = exact_dot(grad_cols.T, grad_full)
    grad_rows = lax.dynamic_slice_in_dim(grad_full, row_start, row_count, 0)
    left_gram = exact_dot(grad_rows, grad_full.T)
    left_next = stat_decay * left_stat[0] + (1.0 - stat_decay) * left_gram
    right_next = stat_decay * right_stat[0] + (1.0 - stat_decay) * right_gram
    full_left, full_right = tuple(
        (
            part.astype(jnp.float32)
            for part in side_by_side(
                (left_next.astype(jnp.bfloat16), right_next.astype(jnp.bfloat16)), REP, 0, 1
            )
        )
    )
    identity = (
        lax.broadcasted_iota(jnp.int32, (size_block, size_block), 0)
        == lax.broadcasted_iota(jnp.int32, (size_block, size_block), 1)
    ).astype(jnp.float32)
    identity_rows = (
        lax.broadcasted_iota(jnp.int32, (row_count, size_block), 0) + row_start
        == lax.broadcasted_iota(jnp.int32, (row_count, size_block), 1)
    ).astype(jnp.float32)
    frob_norms = [
        jnp.sqrt(jnp.sum(full_left * full_left)),
        jnp.sqrt(jnp.sum(full_right * full_right)),
    ]
    root_scales = [jnp.sqrt(jnp.sqrt(frob_norms[0])), jnp.sqrt(jnp.sqrt(frob_norms[1]))]
    iterate_full = [full_left / frob_norms[0], full_right / frob_norms[1]]
    iterate_rows = [left_next / frob_norms[0], right_next / frob_norms[1]]
    roots = [identity_rows, identity_rows]
    for sweep_index in range(ITERS):
        factor_full = [
            (5.0 * identity - iterate_full[0]) * 0.25,
            (5.0 * identity - iterate_full[1]) * 0.25,
        ]
        factor_rows = [
            (5.0 * identity_rows - iterate_rows[0]) * 0.25,
            (5.0 * identity_rows - iterate_rows[1]) * 0.25,
        ]
        for which_side in range(2):
            if sweep_index == 0:
                roots[which_side] = factor_rows[which_side] / root_scales[which_side]
            else:
                roots[which_side] = exact_dot(roots[which_side], factor_full[which_side])
        if sweep_index + 1 < ITERS:
            next_rows = []
            for which_side in range(2):
                whole_factor = factor_full[which_side]
                power_rows = exact_dot(
                    exact_dot(exact_dot(factor_rows[which_side], whole_factor), whole_factor),
                    whole_factor,
                )
                next_rows.append(exact_dot(power_rows, iterate_full[which_side]))
            gathered = tuple(
                (
                    part.astype(jnp.float32)
                    for part in side_by_side_2(
                        (next_rows[0].astype(jnp.bfloat16), next_rows[1].astype(jnp.bfloat16)),
                        REP,
                        0,
                        1,
                    )
                )
            )
            iterate_full = [gathered[0], gathered[1]]
            iterate_rows = next_rows
    right_root_full = collect(roots[1].astype(jnp.bfloat16), REP, 0).astype(jnp.float32)
    precond_rows = exact_dot(exact_dot(roots[0], grad_full), right_root_full)
    square_sums = (
        one_axis_at_a_time(jnp.sum(precond_rows * precond_rows), REP_BLK),
        one_axis_at_a_time(jnp.sum(grad_cols * grad_cols), REP_BLK),
    )
    graft_scale = jnp.sqrt(square_sums[1]) / jnp.sqrt(square_sums[0])
    moment_rows = moment_decay * momentum[0] + graft_scale * precond_rows
    weight_rows = (master[0] - step_size * moment_rows).astype(jnp.bfloat16)
    weight_full = collect(weight_rows, REP, 0)
    returned = lax.all_to_all(
        weight_full.reshape(owners, sub_rows, size_block),
        BLK,
        split_axis=0,
        concat_axis=2,
        tiled=True,
    )
    params = returned.reshape(sub_rows, gradients.shape[2], gradients.shape[3])
    return (params, moment_rows[None], left_next[None], right_next[None])


def solution(mesh):
    split = Mesh(mesh.devices.reshape(4, 2, 2, 4, 8), ("rep_0", "rep_1", "blk_0", "blk_1", "blk_2"))
    in_specs = (
        P(REP, BLK, None, None),
        P(BLK, REP, None),
        P(BLK, REP, None),
        P(BLK, REP, None),
        P(BLK, REP, None),
    )
    out_specs = (P(BLK, None, None), P(BLK, REP, None), P(BLK, REP, None), P(BLK, REP, None))
    return jax.shard_map(
        on_device, mesh=split, in_specs=in_specs, out_specs=out_specs, check_vma=False
    )
```

profile of v0, /device:TPU:8, one launch (start us, length us, event | category | flops | bytes accessed | tf_op | source)
XLA Modules:
  0.0 379.9 jit_solution(4657990853374481389)
XLA Ops:
  7.2 2.1 reshape.49
  10.2 22.4 %all_to_all.59 = bf16[8,2,16384]{2,1,0:T(2,128)(2,1)S(1)} all-to-all(bf16[8,2,16384]{2,1,0:T(2,128)(2,1)S(1)} %reshape.56), channel_id=1, replica_groups=mesh['rep_0'=4,'rep_1'=2,'blk_0'=2,'blk_1'=4,'blk_2'=8] {'rep_0','rep_1'}, dimensions={0} | all-to-all | bytes 1048576 | tf_op jit(solution)/shard_map/all_to_all | solution.py:25
  33.8 30.5 %all_to_all.60 = f32[64,1,512]{2,1,0:T(1,128)S(1)} all-to-all(f32[64,1,512]{2,1,0:T(1,128)S(1)} %reshape.58), channel_id=1, replica_groups=mesh['rep_0'=4,'rep_1'=2,'blk_0'=2,'blk_1'=4,'blk_2'=8] {'blk_0','blk_1'..., dimensions={0} | all-to-all | bytes 262144 | tf_op jit(solution)/shard_map/all_to_all | solution.py:81
  64.8 0.9 reduce.1
  66.0 1.1 broadcast_in_dim.27
  67.1 3.7 all-to-all-start.2
  71.1 26.2 %all-to-all-done.2 = f32[8,512,64]{1,2,0:T(8,128)S(1)} async-done(((f32[8,512,64]{1,2,0:T(8,128)}), f32[8,512,64]{1,2,0:T(8,128)S(1)}, u32[]{:S(2)}, u32[]{:S(2)}) %all-to-all-start.2) | async-done | bytes 1048608 | tf_op jit(solution)/shard_map/all_to_all | solution.py:37
  97.3 1.2 fusion.238
  100.0 31.6 %all-gather.2.cloned.1.call-done = bf16[512,1024]{1,0:T(8,128)(2,1)} async-done(((bf16[64,1024]{1,0:T(8,128)(2,1)}), bf16[512,1024]{1,0:T(8,128)(2,1)}) %all-gather.2.cloned.1.call-update) | async-done | bytes 1048592 | tf_op jit(solution)/shard_map/all_gather | solution.py:47
  131.6 2.2 fusion.2
  135.2 0.9 fusion.225
  136.1 0.9 fusion.235
  137.0 0.9 fusion.233
  138.7 0.9 fusion.223
  139.7 0.9 fusion.230
  140.6 0.9 fusion.228
  142.4 29.0 %all_to_all.61 = bf16[8,64,1024]{2,1,0:T(8,128)(2,1)S(1)} all-to-all(bf16[8,64,1024]{2,1,0:T(8,128)(2,1)S(1)} %broadcast_in_dim.28), channel_id=1, replica_groups=mesh['rep_0'=4,'rep_1'=2,'blk_0'=2,'blk_1'=4,'blk_2'=8] {'rep_0','rep_1'}, dimensions={0} | all-to-all | bytes 2097152 | tf_op jit(solution)/shard_map/all_to_all | solution.py:37
  171.4 0.9 fusion.45
  172.3 0.9 fusion.43
  174.0 0.9 fusion.39
  174.9 0.9 fusion.37
  177.6 29.0 %all_to_all.62 = bf16[8,64,1024]{2,1,0:T(8,128)(2,1)S(1)} all-to-all(bf16[8,64,1024]{2,1,0:T(8,128)(2,1)S(1)} %broadcast_in_dim.29), channel_id=1, replica_groups=mesh['rep_0'=4,'rep_1'=2,'blk_0'=2,'blk_1'=4,'blk_2'=8] {'rep_0','rep_1'}, dimensions={0} | all-to-all | bytes 2097152 | tf_op jit(solution)/shard_map/all_to_all | solution.py:37
  206.6 0.9 fusion.29
  207.5 0.9 fusion.23
  208.4 0.9 fusion.21
  209.2 0.9 fusion.19
  210.5 0.9 fusion.27
  211.4 0.9 fusion.25
  212.6 1.2 broadcast_in_dim.30
  213.8 4.5 %all-to-all-start.5 = ((bf16[8,64,1024]{2,1,0:T(8,128)(2,1)}), bf16[8,64,1024]{2,1,0:T(8,128)(2,1)}, u32[]{:S(2)}, u32[]{:S(2)}) async-start(bf16[8,64,1024]{2,1,0:T(8,128)(2,1)} %broadcast_in_dim.30), calls=%async_computation.5 | async-start | bytes 2097152 | tf_op jit(solution)/shard_map/all_to_all | solution.py:37
  219.2 0.9 fusion.33
  220.1 0.9 fusion.17
  220.9 23.7 %all-to-all-done.5 = bf16[8,64,1024]{2,1,0:T(8,128)(2,1)} async-done(((bf16[8,64,1024]{2,1,0:T(8,128)(2,1)}), bf16[8,64,1024]{2,1,0:T(8,128)(2,1)}, u32[]{:S(2)}, u32[]{:S(2)}) %all-to-all-start.5) | async-done | bytes 1048608 | tf_op jit(solution)/shard_map/all_to_all | solution.py:37
  244.6 1.9 convolution_convert_fusion
  247.4 4.1 %all-to-all-start.6 = ((bf16[8,64,512]{2,1,0:T(8,128)(2,1)}), bf16[8,64,512]{2,1,0:T(8,128)(2,1)}, u32[]{:S(2)}, u32[]{:S(2)}) async-start(bf16[8,64,512]{2,1,0:T(8,128)(2,1)} %broadcast_in_dim.31), calls=%async_computation.6 | async-start | bytes 1048576 | tf_op jit(solution)/shard_map/all_to_all | solution.py:37
  251.5 0.9 fusion.47
  253.3 1.9 fusion.11
  255.2 1.1 fusion.245
  256.3 10.5 %all-to-all-done.6 = bf16[8,64,512]{2,1,0:T(8,128)(2,1)} async-done(((bf16[8,64,512]{2,1,0:T(8,128)(2,1)}), bf16[8,64,512]{2,1,0:T(8,128)(2,1)}, u32[]{:S(2)}, u32[]{:S(2)}) %all-to-all-start.6) | async-done | bytes 524320 | tf_op jit(solution)/shard_map/all_to_all | solution.py:37
  266.8 2.1 multiply_reduce_fusion
  268.9 10.2 %all-reduce.2 = (f32[]{:T(128)}, f32[]{:T(128)}) all-reduce(f32[]{:T(128)} %fusion.133, f32[]{:T(128)} %get-tuple-element.30), channel_id=1, replica_groups=mesh['rep_0'=4,'rep_1'=2,'blk_0'=2,'blk_1'=4,'blk_2'=8] {'rep_0'}, use_global_device_ids=true, to_apply=%region_2.0 | all-reduce | flops 2 | bytes 16 | tf_op jit(solution)/shard_map/psum | solution.py:60
  279.1 3.1 all-reduce.4
  282.2 9.5 %all-reduce.3 = (f32[]{:T(128)}, f32[]{:T(128)}) all-reduce(f32[]{:T(128)} %get-tuple-element.14, f32[]{:T(128)} %get-tuple-element.15), channel_id=1, replica_groups=mesh['rep_0'=4,'rep_1'=2,'blk_0'=2,'blk_1'=4,'blk_2'=8] {'blk_0'}, use_global_device_ids=true, to_apply=%region_4.0 | all-reduce | flops 2 | bytes 16 | tf_op jit(solution)/shard_map/psum | solution.py:60
  291.7 10.9 %all-reduce.1 = (f32[]{:T(128)}, f32[]{:T(128)}) all-reduce(f32[]{:T(128)} %get-tuple-element.12, f32[]{:T(128)} %get-tuple-element.13), channel_id=1, replica_groups=mesh['rep_0'=4,'rep_1'=2,'blk_0'=2,'blk_1'=4,'blk_2'=8] {'blk_1'}, use_global_device_ids=true, to_apply=%region_5.0 | all-reduce | flops 2 | bytes 16 | tf_op jit(solution)/shard_map/psum | solution.py:60
  302.6 16.3 %all-reduce = (f32[]{:T(128)}, f32[]{:T(128)}) all-reduce(f32[]{:T(128)} %get-tuple-element.8, f32[]{:T(128)} %get-tuple-element.9), channel_id=1, replica_groups=mesh['rep_0'=4,'rep_1'=2,'blk_0'=2,'blk_1'=4,'blk_2'=8] {'blk_2'}, use_global_device_ids=true, to_apply=%region_6.0 | all-reduce | flops 2 | bytes 16 | tf_op jit(solution)/shard_map/psum | solution.py:60
  321.1 17.7 %all_to_all.63 = bf16[8,64,512]{2,1,0:T(8,128)(2,1)S(1)} all-to-all(bf16[8,64,512]{2,1,0:T(8,128)(2,1)S(1)} %broadcast_in_dim.32), channel_id=1, replica_groups=mesh['rep_0'=4,'rep_1'=2,'blk_0'=2,'blk_1'=4,'blk_2'=8] {'rep_0','rep_1'}, dimensions={0} | all-to-all | bytes 1048576 | tf_op jit(solution)/shard_map/all_to_all | solution.py:37
  338.8 33.1 %all_to_all.64 = bf16[64,8,512]{2,1,0:T(8,128)(2,1)S(1)} all-to-all(bf16[64,8,512]{2,1,0:T(8,128)(2,1)S(1)} %bitcast.108), channel_id=1, replica_groups=mesh['rep_0'=4,'rep_1'=2,'blk_0'=2,'blk_1'=4,'blk_2'=8] {'blk_0','blk_1'..., dimensions={0} | all-to-all | bytes 1048576 | tf_op jit(solution)/shard_map/all_to_all | solution.py:160
  372.1 1.0 reshape.55
  (50 shorter events, 13.1 us)
Async XLA Ops:
  67.1 30.2 %copy-start.1 = (f32[1,64,512]{2,1,0:T(8,128)S(1)}, f32[1,64,512]{2,1,0:T(8,128)}, u32[]{:S(2)}) copy-start(f32[1,64,512]{2,1,0:T(8,128)} %param.7) | copy-start | bytes 393220
  67.1 30.2 %all-to-all-start.2 = ((f32[8,512,64]{1,2,0:T(8,128)}), f32[8,512,64]{1,2,0:T(8,128)S(1)}, u32[]{:S(2)}, u32[]{:S(2)}) async-start(f32[8,512,64]{1,2,0:T(8,128)} %broadcast_in_dim.27), calls=%async_computation.2 | async-start | bytes 2097152 | tf_op jit(solution)/shard_map/all_to_all | solution.py:37
  70.8 27.7 %copy-start.2 = (f32[1,64,512]{2,1,0:T(8,128)S(1)}, f32[1,64,512]{2,1,0:T(8,128)}, u32[]{:S(2)}) copy-start(f32[1,64,512]{2,1,0:T(8,128)} %param.6) | copy-start | bytes 393220
  70.8 60.8 %all-gather.2.cloned.1.call-start = ((), (), s32[]{:S(2)}) async-start(), calls=%async_computation.9 | async-start | bytes 1179648 | tf_op jit(solution)/shard_map/all_gather | solution.py:47
  98.5 120.6 %copy-start.3 = (f32[64,512]{1,0:T(8,128)}, f32[64,512]{1,0:T(8,128)S(1)}, u32[]{:S(2)}) copy-start(f32[64,512]{1,0:T(8,128)S(1)} %get-tuple-element.19) | copy-start | bytes 393220
  99.3 36.8 %copy-start.4 = (f32[64,512]{1,0:T(8,128)}, f32[64,512]{1,0:T(8,128)S(1)}, u32[]{:S(2)}) copy-start(f32[64,512]{1,0:T(8,128)S(1)} %get-tuple-element.21) | copy-start | bytes 393220
  131.6 3.6 copy-start
  213.8 30.8 %all-to-all-start.5 = ((bf16[8,64,1024]{2,1,0:T(8,128)(2,1)}), bf16[8,64,1024]{2,1,0:T(8,128)(2,1)}, u32[]{:S(2)}, u32[]{:S(2)}) async-start(bf16[8,64,1024]{2,1,0:T(8,128)(2,1)} %broadcast_in_dim.30), calls=%async_computation.5 | async-start | bytes 2097152 | tf_op jit(solution)/shard_map/all_to_all | solution.py:37
  246.5 5.0 %copy-start.5 = (f32[64,512]{1,0:T(8,128)S(1)}, f32[64,512]{1,0:T(8,128)}, u32[]{:S(2)}) copy-start(f32[64,512]{1,0:T(8,128)} %copy-done.4) | copy-start | bytes 393220
  247.4 19.5 %all-to-all-start.6 = ((bf16[8,64,512]{2,1,0:T(8,128)(2,1)}), bf16[8,64,512]{2,1,0:T(8,128)(2,1)}, u32[]{:S(2)}, u32[]{:S(2)}) async-start(bf16[8,64,512]{2,1,0:T(8,128)(2,1)} %broadcast_in_dim.31), calls=%async_computation.6 | async-start | bytes 1048576 | tf_op jit(solution)/shard_map/all_to_all | solution.py:37
  255.2 65.1 %copy-start.6 = (f32[1,64,512]{2,1,0:T(8,128)S(1)}, f32[1,64,512]{2,1,0:T(8,128)}, u32[]{:S(2)}) copy-start(f32[1,64,512]{2,1,0:T(8,128)} %param.8) | copy-start | bytes 393220
  255.2 65.1 %copy-start.7 = (f32[1,64,512]{2,1,0:T(8,128)S(1)}, f32[1,64,512]{2,1,0:T(8,128)}, u32[]{:S(2)}) copy-start(f32[1,64,512]{2,1,0:T(8,128)} %param.9) | copy-start | bytes 393220
Sparse Core Ops, SparseCore 0:
  100.1 31.4 all-gather.1
where the time goes:
time: 381 us; the launch traced here: 380 us
  blocking collectives  212 us (56%)
  waiting for transfers between devices  92 us (24%)
  matrix products  31.6 us (8%)
  between operations  17.3 us (5%)
  starting transfers between devices  12.5 us (3%)
  local copies, waits for them, and re-layouts  9.36 us (2%)
  other arithmetic  5.43 us (1%)
    all_to_all x3, blocking collectives, sent_to_all(): return lax.all_to_all(copies, axis, split_axis=0, concat_axis=0, tiled=True)  75.7 us
    all_to_all x3, waiting for transfers between devices, sent_to_all(): return lax.all_to_all(copies, axis, split_axis=0, concat_axis=0, tiled=True)  60.4 us
    psum x5, blocking collectives, one_axis_at_a_time(): shard = lax.psum(shard, axis)  50 us
    all_to_all x1, blocking collectives, on_device(): lax.all_to_all(weight_full.reshape(owners, sub_rows, size_block), BLK, sp...  33.1 us
    dot_general x34, matrix products, exact_dot(): jnp.dot(left, right, precision=lax.Precision.HIGHEST, preferred_element_t...  31.6 us
    all_gather x1, waiting for transfers between devices, side_by_side(): out = lax.all_gather(both, axis, axis=dim, tiled=True)  31.6 us
    all_to_all x1, blocking collectives, on_device(): lax.all_to_all(summed_rows, BLK, split_axis=1, concat_axis=0, tiled=True)  30.5 us
    all_to_all x1, blocking collectives, summed_on_arrival(): pieces = lax.all_to_all(in_blocks(shard, dim, size), axis, 0, 0, tiled=True)  22.4 us
  transfers between devices with their start and end apart: 4, of which 4 were waited for; matrix products, arithmetic and copies ran while one was open for 2% of the time, Pallas kernels for 0%

commit v1 on v0

v1 whole, which is shorter than its diff:
```python
import functools
import jax
import jax.numpy as jnp
from jax import lax
from jax.experimental import pallas as pl
from jax.experimental.pallas import tpu as pltpu
from jax.sharding import Mesh
from jax.sharding import PartitionSpec as P

REP = ("zl", "co")
COL = ("zh", "x")
BLK = ("zh", "x", "y")
ALL = ("zl", "co", "zh", "x", "y")
FAN = ("zl", "zh", "x")
SIZES = (4, 2, 2, 4, 8)
N = 8
ROWS = 64
BLOCK = 512
ITERS = 4
LANES = 128
WIDE = BLOCK // LANES

stat_decay = 0.9
moment_decay = 0.9
step_size = 0.25

F32 = jnp.float32
BF16 = jnp.bfloat16


def exchanged(pieces, axis):
    return lax.all_to_all(pieces, axis, split_axis=0, concat_axis=0, tiled=True)


def rep_with_y():
    return [
        ((r * N + c) * N + y, (y * N + c) * N + r)
        for r in range(N)
        for c in range(N)
        for y in range(N)
    ]


def three_parts(value):
    high = value.astype(BF16).astype(F32)
    rest = value - high
    middle = rest.astype(BF16).astype(F32)
    return high, middle, rest - middle


def dot(a, b, dims=((1,), (0,))):
    return lax.dot_general(a, b, (dims, ((), ())), preferred_element_type=F32)


def block_kernel(y_ref, g_ref, side_ref, msg_ref, ret_ref, m_f, m_b, v_b, w_f, w_b, g_b, y_f, y_b, z_b):
    own = pl.multiple_of(y_ref[0] * ROWS, ROWS)
    chunk = BLOCK // 2
    spans = [pl.ds(k * chunk, chunk) for k in range(2)]
    norm_g = jnp.zeros((1, 1), F32)
    for rows in spans:
        part = g_ref[rows, :]
        norm_g += jnp.sum(part * part, keepdims=True)
        g_b[rows, :] = part.astype(BF16)
        y_f[rows, :] = part
        y_b[rows, :] = part.astype(BF16)
    scale = jnp.ones((1, 1), F32)
    for side in range(2):
        gram = dot(g_b[...], g_b[...], (((1,), (1,)), ((0,), (0,)))[side])
        w_f[side] = gram
        ret_ref[pl.ds((1 + side) * ROWS, ROWS), :] = w_f[side, pl.ds(own, ROWS), :].astype(BF16)
        total = jnp.zeros((1, 1), F32)
        for k in range(N):
            rows = pl.ds(k * ROWS, ROWS)
            old = side_ref[k, side * ROWS : (side + 1) * ROWS, :].astype(F32)
            new = stat_decay * old + (1.0 - stat_decay) * w_f[side, rows, :]
            m_f[side, rows, :] = new
            total += jnp.sum(new * new, keepdims=True)
        frob = jnp.sqrt(total)
        scale = scale / jnp.sqrt(jnp.sqrt(frob))
        inverse = 1.0 / frob
        for rows in spans:
            new = m_f[side, rows, :] * inverse
            m_f[side, rows, :] = new
            m_b[side, rows, :] = new.astype(BF16)

    def apply_factors():
        for rows in spans:
            new = 1.25 * y_f[rows, :] - 0.25 * dot(m_b[0, rows, :], y_b[...])
            y_f[rows, :] = new
            z_b[rows, :] = new.astype(BF16)
        for rows in spans:
            new = 1.25 * y_f[rows, :] - 0.25 * dot(z_b[rows, :], m_b[1])
            y_f[rows, :] = new
            y_b[rows, :] = new.astype(BF16)

    def sweep(_, carry):
        for side in range(2):
            for rows in spans:
                square = dot(m_b[side, rows, :], m_b[side])
                v_b[side, rows, :] = (0.0625 * square - 0.625 * m_f[side, rows, :]).astype(BF16)
        apply_factors()
        for side in range(2):
            for rows in spans:
                new = 1.5625 * m_f[side, rows, :] + dot(v_b[side, rows, :], m_b[side])
                w_f[side, rows, :] = new
                w_b[side, rows, :] = new.astype(BF16)
        for side in range(2):
            for rows in spans:
                new = 1.5625 * w_f[side, rows, :] + dot(v_b[side, rows, :], w_b[side])
                m_f[side, rows, :] = new
                m_b[side, rows, :] = new.astype(BF16)
        return carry

    lax.fori_loop(0, ITERS - 1, sweep, 0)
    apply_factors()
    norm_p = jnp.zeros((1, 1), F32)
    for rows in spans:
        new = y_f[rows, :] * scale
        norm_p += jnp.sum(new * new, keepdims=True)
        y_f[rows, :] = new
    ret_ref[0:ROWS, :] = y_f[pl.ds(own, ROWS), :].astype(BF16)
    lane = lax.broadcasted_iota(jnp.int32, (16, LANES), 1)
    norms = jnp.zeros((16, LANES), F32)
    for k, part in enumerate(three_parts(norm_p) + three_parts(norm_g)):
        norms = jnp.where(lane == k, part, norms)
    norms = norms.astype(BF16)
    start = y_ref[0] * N
    for c in range(N):
        rows = y_f[pl.ds(pl.multiple_of(c * ROWS + start, N), N), :]
        both = jnp.concatenate([rows, side_ref[c, 2 * ROWS : 2 * ROWS + N, :].astype(F32)], axis=0)
        both = both.astype(BF16)
        for z in range(SIZES[0]):
            msg_ref[z * N + c, :, 0:BLOCK] = both
            msg_ref[z * N + c, :, BLOCK : BLOCK + LANES] = norms


def final_kernel(got_ref, ret_ref, mom_ref, params_ref, mom_out_ref, rows_f):
    total = jnp.zeros((16, LANES), F32)
    for q in range(2):
        for z in range(SIZES[0]):
            for i in range(N):
                total += got_ref[q, z * N + i, :, BLOCK : BLOCK + LANES].astype(F32)
    lane = lax.broadcasted_iota(jnp.int32, (16, LANES), 1)
    norm_p = jnp.sum(jnp.where(lane < 3, total, 0.0), keepdims=True) * (1.0 / 16)
    norm_g = jnp.sum(jnp.where(lane < 3, 0.0, total), keepdims=True) * (1.0 / 16)
    graft = jnp.sqrt(norm_g) / jnp.sqrt(norm_p)
    for z in range(SIZES[0]):
        for q in range(2):
            slot = (z * 2 + q) % 2
            for i in range(N):
                both = got_ref[q, z * N + i, :, 0:BLOCK].astype(F32)
                both = both[N:, :] - step_size * (graft * both[:N, :])
                for w in range(WIDE):
                    rows_f[slot, w, i * N : (i + 1) * N, :] = both[:, w * LANES : (w + 1) * LANES]
            for p in range(N):
                for w in range(WIDE):
                    cols = pl.ds((z * 2 + q) * BLOCK + w * LANES, LANES)
                    params_ref[p, :, cols] = rows_f[slot, w, pl.ds(p, N, stride=N), :].astype(BF16)
    mom_out_ref[...] = moment_decay * mom_ref[...] + graft * ret_ref[0:ROWS, :].astype(F32)


def vmem(count):
    return [pl.BlockSpec(memory_space=pltpu.VMEM)] * count


def on_device(gradients, left_stat, right_stat, momentum, master):
    y = lax.axis_index("y")
    base = (master[0] - (step_size * moment_decay) * momentum[0]).astype(BF16)
    side = jnp.concatenate([left_stat[0].astype(BF16), right_stat[0].astype(BF16), base], axis=0)
    side = lax.ppermute(side, ALL, rep_with_y())
    stats = jnp.broadcast_to(side[None, : 2 * ROWS], (N, 2 * ROWS, BLOCK))
    side = jnp.concatenate([stats, side[2 * ROWS :].reshape(N, N, BLOCK)], axis=1)
    side = exchanged(side, "y")

    pieces = gradients.reshape(N, N, N, BLOCK).transpose(2, 0, 1, 3)
    pieces = exchanged(pieces, REP)
    mean = jnp.sum(pieces.astype(F32), axis=0) * (1.0 / N)
    mean = mean.transpose(1, 0, 2)
    mean = jnp.broadcast_to(mean[:, None], (N, N, N, BLOCK)).reshape(N * N, N, BLOCK)
    mean = exchanged(mean, BLK).reshape(BLOCK, BLOCK)

    messages, ret = pl.pallas_call(
        block_kernel,
        out_shape=(
            jax.ShapeDtypeStruct((SIZES[0] * N, 16, BLOCK + LANES), BF16),
            jax.ShapeDtypeStruct((3 * ROWS, BLOCK), BF16),
        ),
        in_specs=[pl.BlockSpec(memory_space=pltpu.SMEM)] + vmem(2),
        out_specs=tuple(vmem(2)),
        scratch_shapes=[
            pltpu.VMEM((2, BLOCK, BLOCK), F32),
            pltpu.VMEM((2, BLOCK, BLOCK), BF16),
            pltpu.VMEM((2, BLOCK, BLOCK), BF16),
            pltpu.VMEM((2, BLOCK, BLOCK), F32),
            pltpu.VMEM((2, BLOCK, BLOCK), BF16),
            pltpu.VMEM((BLOCK, BLOCK), BF16),
            pltpu.VMEM((BLOCK, BLOCK), F32),
            pltpu.VMEM((BLOCK, BLOCK), BF16),
            pltpu.VMEM((BLOCK, BLOCK), BF16),
        ],
        compiler_params=pltpu.CompilerParams(vmem_limit_bytes=32 * 1024 * 1024),
        cost_estimate=pl.CostEstimate(flops=28 * 2 * BLOCK**3, bytes_accessed=4 << 20, transcendentals=0),
        name="block_update",
    )(y.astype(jnp.int32).reshape(1), mean, side)

    ret = lax.ppermute(ret, ALL, rep_with_y())
    got = exchanged(messages, FAN)
    got = exchanged(jnp.broadcast_to(got[None], (2, *got.shape)), "co")

    params, moment_rows = pl.pallas_call(
        final_kernel,
        out_shape=(
            jax.ShapeDtypeStruct((N, N, N * BLOCK), BF16),
            jax.ShapeDtypeStruct((ROWS, BLOCK), F32),
        ),
        in_specs=vmem(3),
        out_specs=tuple(vmem(2)),
        scratch_shapes=[pltpu.VMEM((2, WIDE, ROWS, LANES), F32)],
        compiler_params=pltpu.CompilerParams(vmem_limit_bytes=16 * 1024 * 1024),
        name="weights",
    )(got.reshape(2, SIZES[0] * N, 16, BLOCK + LANES), ret, momentum[0])
    left_next = stat_decay * left_stat[0] + (1.0 - stat_decay) * ret[ROWS : 2 * ROWS].astype(F32)
    right_next = stat_decay * right_stat[0] + (1.0 - stat_decay) * ret[2 * ROWS :].astype(F32)
    return (params, moment_rows[None], left_next[None], right_next[None])


def solution(mesh):
    split = Mesh(mesh.devices.reshape(SIZES), ALL)
    in_specs = (P(REP, BLK, None, None),) + (P(BLK, REP, None),) * 4
    out_specs = (P(BLK, None, None),) + (P(BLK, REP, None),) * 3
    return jax.shard_map(
        on_device, mesh=split, in_specs=in_specs, out_specs=out_specs, check_vma=False
    )
```

time: 381 us -> 172 us (0.45)
  blocking collectives: 212 us -> 4.79 us
  matrix products: 31.6 us -> 0 us
  starting transfers between devices: 12.5 us -> 39 us
  waiting for transfers between devices: 92 us -> 109 us
  between operations: 17.3 us -> 0.79 us
  Pallas kernels: 0 us -> 11.8 us
  local copies, waits for them, and re-layouts: 9.36 us -> 3.58 us
    all_to_all x6 -> x1, blocking collectives: 162 us -> 4.79 us  [exchanged(): return lax.all_to_all(pieces, axis, split_axis=0, concat_axis=0, tiled=True)]
    psum x5 -> x0, blocking collectives: 50 us -> none  [one_axis_at_a_time(): shard = lax.psum(shard, axis)]
    all_to_all x3 -> x4, waiting for transfers between devices: 60.4 us -> 101 us  [exchanged(): return lax.all_to_all(pieces, axis, split_axis=0, concat_axis=0, tiled=True)]
    dot_general x34 -> x0, matrix products: 31.6 us -> none  [exact_dot(): jnp.dot(left, right, precision=lax.Precision.HIGHEST, preferred_element_t...]
    all_gather x1 -> x0, waiting for transfers between devices: 31.6 us -> none  [side_by_side(): out = lax.all_gather(both, axis, axis=dim, tiled=True)]
    all_to_all x3 -> x4, starting transfers between devices: 12.3 us -> 33.2 us  [exchanged(): return lax.all_to_all(pieces, axis, split_axis=0, concat_axis=0, tiled=True)]
    pallas_call x0 -> x2, Pallas kernels: none -> 11.8 us  [the longest x1 10.4 us: on_device(): pl.pallas_call(block_kernel, out_shape=(jax.ShapeDtypeStruct((SIZES[0] *...]
    ppermute x0 -> x2, waiting for transfers between devices: none -> 8.4 us  [the longest x1 5.06 us: on_device(): ret = lax.ppermute(ret, ALL, rep_with_y())]
  transfers between devices with their start and end apart: 4 -> 6, of which waited for: 4 -> 6; matrix products, arithmetic and copies ran while one was open for 2% -> 1% of each run, Pallas kernels for 0% -> 0%
where the time goes in v1:
time: 172 us; the launch traced here: 171 us
  waiting for transfers between devices  109 us (63%)
  starting transfers between devices  39 us (23%)
  Pallas kernels  11.8 us (7%)
  blocking collectives  4.79 us (3%)
  local copies, waits for them, and re-layouts  3.58 us (2%)
  other arithmetic  1.95 us (1%)
    all_to_all x4, waiting for transfers between devices, exchanged(): return lax.all_to_all(pieces, axis, split_axis=0, concat_axis=0, tiled=True)  101 us
    all_to_all x4, starting transfers between devices, exchanged(): return lax.all_to_all(pieces, axis, split_axis=0, concat_axis=0, tiled=True)  33.2 us
    pallas_call x1, Pallas kernels, on_device(): pl.pallas_call(block_kernel, out_shape=(jax.ShapeDtypeStruct((SIZES[0] *...  10.4 us
    ppermute x1, waiting for transfers between devices, on_device(): ret = lax.ppermute(ret, ALL, rep_with_y())  5.06 us
    all_to_all x1, blocking collectives, exchanged(): return lax.all_to_all(pieces, axis, split_axis=0, concat_axis=0, tiled=True)  4.79 us
    ppermute x1, starting transfers between devices, on_device(): side = lax.ppermute(side, ALL, rep_with_y())  3.94 us
  transfers between devices with their start and end apart: 6, of which 6 were waited for; matrix products, arithmetic and copies ran while one was open for 1% of the time, Pallas kernels for 0%

profile of v1, /device:TPU:8, one launch (start us, length us, event | category | flops | bytes accessed | tf_op | source)
XLA Modules:
  0.0 171.3 jit_solution(12588886804773178700)
XLA Ops:
  0.6 1.2 copy.17
  1.8 0.0 copy-start
  1.9 0.0 copy-start.3
  1.9 0.0 copy-start.1
  1.9 0.0 copy-start.2
  1.9 0.9 copy.11
  2.8 7.3 %all-to-all-start = ((bf16[8,8,8,512]{3,2,1,0:T(8,128)(2,1)}), bf16[8,8,8,512]{3,2,1,0:T(8,128)(2,1)S(1)}, u32[]{:S(2)}, u32[]{:S(2)}) async-start(bf16[8,8,8,512]{3,2,1,0:T(8,128)(2,1)} %copy.11), calls=%async_computation | async-start | bytes 1048576 | tf_op jit(solution)/shard_map/all_to_all | solution.py:32
  10.1 0.0 copy-done
  10.1 0.0 copy-done.3
  10.2 0.0 copy-done.1
  10.2 0.0 copy-done.2
  10.2 3.9 %collective-permute-start = (bf16[192,512]{1,0:T(8,128)(2,1)S(1)}, bf16[192,512]{1,0:T(8,128)(2,1)S(1)}, u32[]{:S(2)}, u32[]{:S(2)}) collective-permute-start(bf16[192,512]{1,0:T(8,128)(2,1)S(1)} %pad_maximum_fusion.1), channel_id=1, source_target_pairs={{0,0},{1,64},{2,128},{3,192},{4,256},{5,320},{6,384},{7,448},{8,8}... | collective-permute-start | bytes 589832 | tf_op jit(solution)/shard_map/ppermute | solution.py:170
  14.2 3.3 %collective-permute-done = bf16[192,512]{1,0:T(8,128)(2,1)S(1)} collective-permute-done((bf16[192,512]{1,0:T(8,128)(2,1)S(1)}, bf16[192,512]{1,0:T(8,128)(2,1)S(1)}, u32[]{:S(2)}, u32[]{:S(2)}) %collective-permute-start) | collective-permute-done | bytes 196640 | tf_op jit(solution)/shard_map/ppermute | solution.py:170
  17.5 0.1 broadcast_in_dim.13
  17.6 1.1 pad_maximum_fusion
  18.7 13.7 %all-to-all-done = bf16[8,8,8,512]{3,2,1,0:T(8,128)(2,1)S(1)} async-done(((bf16[8,8,8,512]{3,2,1,0:T(8,128)(2,1)}), bf16[8,8,8,512]{3,2,1,0:T(8,128)(2,1)S(1)}, u32[]{:S(2)}, u32[]{:S(2)}) %all-to-all-start) | async-done | bytes 524320 | tf_op jit(solution)/shard_map/all_to_all | solution.py:32
  32.4 9.0 %all-to-all-start.2 = ((bf16[8,136,512]{2,1,0:T(8,128)(2,1)}), bf16[8,136,512]{2,1,0:T(8,128)(2,1)S(1)}, u32[]{:S(2)}, u32[]{:S(2)}) async-start(bf16[8,136,512]{2,1,0:T(8,128)(2,1)} %pad_maximum_fusion), calls=%async_computation.2 | async-start | bytes 2228224 | tf_op jit(solution)/shard_map/all_to_all | solution.py:32
  41.4 0.1 convert_reduce_fusion
  41.5 0.1 copy.13
  41.6 28.2 %all-to-all-done.2.side_ref = bf16[8,136,512]{2,1,0:T(8,128)(2,1)S(1)} async-done(((bf16[8,136,512]{2,1,0:T(8,128)(2,1)}), bf16[8,136,512]{2,1,0:T(8,128)(2,1)S(1)}, u32[]{:S(2)}, u32[]{:S(2)}) %all-to-all-start.2) | async-done | bytes 1114144 | tf_op jit(solution)/shard_map/all_to_all | solution.py:32
  69.8 1.1 broadcast_in_dim.12
  70.9 12.1 %all-to-all-start.1 = ((f32[64,8,512]{2,1,0:T(8,128)}), f32[64,8,512]{2,1,0:T(8,128)S(1)}, u32[]{:S(2)}, u32[]{:S(2)}) async-start(f32[64,8,512]{2,1,0:T(8,128)} %bitcast.3), calls=%async_computation.1 | async-start | bytes 2097152 | tf_op jit(solution)/shard_map/all_to_all | solution.py:32
  83.0 33.3 %all-to-all-done.1 = f32[64,8,512]{2,1,0:T(8,128)S(1)} async-done(((f32[64,8,512]{2,1,0:T(8,128)}), f32[64,8,512]{2,1,0:T(8,128)S(1)}, u32[]{:S(2)}, u32[]{:S(2)}) %all-to-all-start.1) | async-done | bytes 1048608 | tf_op jit(solution)/shard_map/all_to_all | solution.py:32
  116.3 10.4 %block_update.1 = (bf16[32,16,640]{2,1,0:T(8,128)(2,1)}, bf16[192,512]{1,0:T(8,128)(2,1)S(1)}) custom-call(s32[1]{0:T(128)} %bitcast.y_ref, f32[512,512]{1,0:T(8,128)S(1)} %bitcast.40, bf16[8,136,512]{2,1,0:T(8,128)(2,1)S(1)} %all-to-all-done.2.side_ref), custom_call_target="tpu_custom_call" | custom-call | flops 7516192768 | bytes 4194304 | tf_op jit(solution)/shard_map/block_update/pallas_call | solution.py:182
  126.7 4.8 %all-to-all-start.3 = ((bf16[32,16,640]{2,1,0:T(8,128)(2,1)}), bf16[32,16,640]{2,1,0:T(8,128)(2,1)S(1)}, u32[]{:S(2)}, u32[]{:S(2)}) async-start(bf16[32,16,640]{2,1,0:T(8,128)(2,1)} %get-tuple-element.8), calls=%async_computation.3 | async-start | bytes 1310720 | tf_op jit(solution)/shard_map/all_to_all | solution.py:32
  131.5 1.9 %collective-permute-start.1 = (bf16[192,512]{1,0:T(8,128)(2,1)S(1)}, bf16[192,512]{1,0:T(8,128)(2,1)S(1)}, u32[]{:S(2)}, u32[]{:S(2)}) collective-permute-start(bf16[192,512]{1,0:T(8,128)(2,1)S(1)} %get-tuple-element.9), channel_id=1, source_target_pairs={{0,0},{1,64},{2,128},{3,192},{4,256},{5,320},{6,384},{7,448},{8,8}... | collective-permute-start | bytes 589832 | tf_op jit(solution)/shard_map/ppermute | solution.py:206
  133.4 5.1 %collective-permute-done.1.ret_ref = bf16[192,512]{1,0:T(8,128)(2,1)S(1)} collective-permute-done((bf16[192,512]{1,0:T(8,128)(2,1)S(1)}, bf16[192,512]{1,0:T(8,128)(2,1)S(1)}, u32[]{:S(2)}, u32[]{:S(2)}) %collective-permute-start.1) | collective-permute-done | bytes 196640 | tf_op jit(solution)/shard_map/ppermute | solution.py:206
  138.5 0.7 fusion
  139.2 25.8 %all-to-all-done.3 = bf16[32,16,640]{2,1,0:T(8,128)(2,1)S(1)} async-done(((bf16[32,16,640]{2,1,0:T(8,128)(2,1)}), bf16[32,16,640]{2,1,0:T(8,128)(2,1)S(1)}, u32[]{:S(2)}, u32[]{:S(2)}) %all-to-all-start.3) | async-done | bytes 655392 | tf_op jit(solution)/shard_map/all_to_all | solution.py:32
  165.0 0.1 broadcast_in_dim.14
  165.1 4.8 %all_to_all.25.got_ref = bf16[2,32,16,640]{3,2,1,0:T(8,128)(2,1)S(1)} all-to-all(bf16[2,32,16,640]{3,2,1,0:T(8,128)(2,1)S(1)} %broadcast_in_dim.14), channel_id=1, replica_groups=mesh['zl'=4,'co'=2,'zh'=2,'x'=4,'y'=8] {'co'}, dimensions={0} | all-to-all | bytes 2621440 | tf_op jit(solution)/shard_map/all_to_all | solution.py:32
  169.9 1.4 weights.1
  (6 shorter events, 0.1 us)
Async XLA Ops:
  1.8 8.3 %copy-start = (f32[1,64,512]{2,1,0:T(8,128)S(1)}, f32[1,64,512]{2,1,0:T(8,128)}, u32[]{:S(2)}) copy-start(f32[1,64,512]{2,1,0:T(8,128)} %param.8) | copy-start | bytes 393220
  1.9 8.3 %copy-start.3 = (f32[1,64,512]{2,1,0:T(8,128)S(1)}, f32[1,64,512]{2,1,0:T(8,128)}, u32[]{:S(2)}) copy-start(f32[1,64,512]{2,1,0:T(8,128)} %param.9) | copy-start | bytes 393220
  1.9 8.3 %copy-start.1 = (f32[1,64,512]{2,1,0:T(8,128)S(1)}, f32[1,64,512]{2,1,0:T(8,128)}, u32[]{:S(2)}) copy-start(f32[1,64,512]{2,1,0:T(8,128)} %param.7) | copy-start | bytes 393220
  1.9 8.3 %copy-start.2 = (f32[1,64,512]{2,1,0:T(8,128)S(1)}, f32[1,64,512]{2,1,0:T(8,128)}, u32[]{:S(2)}) copy-start(f32[1,64,512]{2,1,0:T(8,128)} %param.6) | copy-start | bytes 393220
  2.8 29.5 %all-to-all-start = ((bf16[8,8,8,512]{3,2,1,0:T(8,128)(2,1)}), bf16[8,8,8,512]{3,2,1,0:T(8,128)(2,1)S(1)}, u32[]{:S(2)}, u32[]{:S(2)}) async-start(bf16[8,8,8,512]{3,2,1,0:T(8,128)(2,1)} %copy.11), calls=%async_computation | async-start | bytes 1048576 | tf_op jit(solution)/shard_map/all_to_all | solution.py:32
  10.2 7.3 %collective-permute-start = (bf16[192,512]{1,0:T(8,128)(2,1)S(1)}, bf16[192,512]{1,0:T(8,128)(2,1)S(1)}, u32[]{:S(2)}, u32[]{:S(2)}) collective-permute-start(bf16[192,512]{1,0:T(8,128)(2,1)S(1)} %pad_maximum_fusion.1), channel_id=1, source_target_pairs={{0,0},{1,64},{2,128},{3,192},{4,256},{5,320},{6,384},{7,448},{8,8}... | collective-permute-start | bytes 589832 | tf_op jit(solution)/shard_map/ppermute | solution.py:170
  32.4 37.4 %all-to-all-start.2 = ((bf16[8,136,512]{2,1,0:T(8,128)(2,1)}), bf16[8,136,512]{2,1,0:T(8,128)(2,1)S(1)}, u32[]{:S(2)}, u32[]{:S(2)}) async-start(bf16[8,136,512]{2,1,0:T(8,128)(2,1)} %pad_maximum_fusion), calls=%async_computation.2 | async-start | bytes 2228224 | tf_op jit(solution)/shard_map/all_to_all | solution.py:32
  70.9 45.4 %all-to-all-start.1 = ((f32[64,8,512]{2,1,0:T(8,128)}), f32[64,8,512]{2,1,0:T(8,128)S(1)}, u32[]{:S(2)}, u32[]{:S(2)}) async-start(f32[64,8,512]{2,1,0:T(8,128)} %bitcast.3), calls=%async_computation.1 | async-start | bytes 2097152 | tf_op jit(solution)/shard_map/all_to_all | solution.py:32
  126.7 38.3 %all-to-all-start.3 = ((bf16[32,16,640]{2,1,0:T(8,128)(2,1)}), bf16[32,16,640]{2,1,0:T(8,128)(2,1)S(1)}, u32[]{:S(2)}, u32[]{:S(2)}) async-start(bf16[32,16,640]{2,1,0:T(8,128)(2,1)} %get-tuple-element.8), calls=%async_computation.3 | async-start | bytes 1310720 | tf_op jit(solution)/shard_map/all_to_all | solution.py:32
  131.5 7.0 %collective-permute-start.1 = (bf16[192,512]{1,0:T(8,128)(2,1)S(1)}, bf16[192,512]{1,0:T(8,128)(2,1)S(1)}, u32[]{:S(2)}, u32[]{:S(2)}) collective-permute-start(bf16[192,512]{1,0:T(8,128)(2,1)S(1)} %get-tuple-element.9), channel_id=1, source_target_pairs={{0,0},{1,64},{2,128},{3,192},{4,256},{5,320},{6,384},{7,448},{8,8}... | collective-permute-start | bytes 589832 | tf_op jit(solution)/shard_map/ppermute | solution.py:206

commit v2 on v1

v2 whole, which is shorter than its diff:
```python
import jax
import jax.numpy as jnp
from jax import lax
from jax.experimental import pallas as pl
from jax.experimental.pallas import tpu as pltpu
from jax.sharding import Mesh
from jax.sharding import PartitionSpec as P

REP = ("zl", "co")
ALL = ("zl", "co", "zh", "x", "y")
BLK = ("zh", "x", "y")
PLANE = ("zh", "y")
SIZES = (4, 2, 2, 4, 8)
N = 8
ROWS = 64
BLOCK = 512
ITERS = 4
LANES = 128
HALF = BLOCK // 2
SHARE = 3 * ROWS
MESSAGE = 40
WIDE = BLOCK // LANES

stat_decay = 0.9
moment_decay = 0.9
step_size = 0.25

F32 = jnp.float32
BF16 = jnp.bfloat16


def exchanged(pieces, axis):
    return lax.all_to_all(pieces, axis, split_axis=0, concat_axis=0, tiled=True)


def moved(shard, move):
    sizes = SIZES

    def place(where):
        index = 0
        for size, value in zip(sizes, where):
            index = index * size + value
        return index

    def device(index):
        where = []
        for size in reversed(sizes):
            where.append(index % size)
            index //= size
        return tuple(reversed(where))

    count = 1
    for size in sizes:
        count *= size
    pairs = [(k, place(move(*device(k)))) for k in range(count)]
    return lax.ppermute(shard, ALL, pairs)


def turned(shard):
    return moved(shard, lambda zl, co, zh, x, y: (x, co, zh, zl, y))


def along_x(shard, flip):
    return moved(shard, lambda zl, co, zh, x, y: (zl, co, zh, x ^ flip, y))


def other_core(shard):
    return moved(shard, lambda zl, co, zh, x, y: (zl, 1 - co, zh, x, y))


def spread(shard, axis):
    copies = jnp.broadcast_to(shard[None], (lax.axis_size(axis), *shard.shape))
    return exchanged(copies, axis)


def three_parts(value):
    high = value.astype(BF16).astype(F32)
    rest = value - high
    middle = rest.astype(BF16).astype(F32)
    return high, middle, rest - middle


def dot(a, b, dims=((1,), (0,))):
    return lax.dot_general(a, b, (dims, ((), ())), preferred_element_type=F32)


def pack_kernel(grad_ref, out_ref, rows_f):
    for j in range(N):
        for w in range(WIDE):
            slot = (j * WIDE + w) % 4
            for p in range(N):
                cols = slice(j * BLOCK + w * LANES, j * BLOCK + (w + 1) * LANES)
                rows_f[slot, p * N : (p + 1) * N, :] = grad_ref[p, :, cols].astype(F32)
            lanes = slice(w % 2 * LANES, (w % 2 + 1) * LANES)
            for i in range(N):
                at = (i // 4 * N + j) * N
                rows = rows_f[slot, pl.ds(i, N, stride=N), :]
                out_ref[i % 4 * 2 + w // 2, at : at + N, lanes] = rows.astype(BF16)


def gram_kernel(own_ref, got_ref, g_ref, gram_ref, ret_ref, g_b):
    own = pl.multiple_of(own_ref[0] * ROWS, ROWS)
    for half in range(2):
        for x in range(4):
            for zh in range(2):
                rows = slice((zh * 4 + x) * ROWS, (zh * 4 + x + 1) * ROWS)
                part = got_ref[half, (x * 2 + zh) * ROWS : (x * 2 + zh + 1) * ROWS, :]
                cols = slice(half * HALF, (half + 1) * HALF)
                g_ref[rows, cols] = part
                g_b[rows, cols] = part.astype(BF16)
    for side in range(2):
        gram_ref[side] = dot(g_b[...], g_b[...], (((1,), (1,)), ((0,), (0,)))[side])
        ret_ref[side * ROWS : (side + 1) * ROWS, :] = gram_ref[side, pl.ds(own, ROWS), :].astype(BF16)


def block_kernel(
    own_ref, g_ref, gram_ref, s0_ref, s1_ref, s2_ref, s3_ref, twin_ref,
    msg_ref, ret_ref, m_f, m_b, v_b, w_f, w_b, y_f, y_b, z_b, base_f,
):
    own = pl.multiple_of(own_ref[0] * ROWS, ROWS)
    x = own_ref[0] >> 1
    co = own_ref[0] & 1
    chunk = BLOCK // 2
    spans = [pl.ds(k * chunk, chunk) for k in range(2)]
    norm_g = jnp.zeros((1, 1), F32)
    for rows in spans:
        part = g_ref[rows, :]
        norm_g += jnp.sum(part * part, keepdims=True)
        y_f[rows, :] = part
        y_b[rows, :] = part.astype(BF16)
    shares = []
    for flip, ref in enumerate((s0_ref, s1_ref, s2_ref, s3_ref)):
        shares.append((pl.multiple_of((own_ref[0] ^ (2 * flip)) * ROWS, ROWS), ref, 0))
        shares.append((pl.multiple_of((own_ref[0] ^ (2 * flip + 1)) * ROWS, ROWS), twin_ref, flip * SHARE))
    scale = jnp.ones((1, 1), F32)
    for side in range(2):
        total = jnp.zeros((1, 1), F32)
        for at, ref, start in shares:
            rows = pl.ds(at, ROWS)
            old = ref[start + side * ROWS : start + (side + 1) * ROWS, :].astype(F32)
            new = stat_decay * old + (1.0 - stat_decay) * gram_ref[side, rows, :]
            m_f[side, rows, :] = new
            total += jnp.sum(new * new, keepdims=True)
        frob = jnp.sqrt(total)
        scale = scale / jnp.sqrt(jnp.sqrt(frob))
        inverse = 1.0 / frob
        for rows in spans:
            new = m_f[side, rows, :] * inverse
            m_f[side, rows, :] = new
            m_b[side, rows, :] = new.astype(BF16)
    for at, ref, start in shares:
        base_f[pl.ds(at, ROWS), :] = ref[start + 2 * ROWS : start + 3 * ROWS, :].astype(F32)

    def apply_factors():
        for rows in spans:
            new = 1.25 * y_f[rows, :] - 0.25 * dot(m_b[0, rows, :], y_b[...])
            y_f[rows, :] = new
            z_b[rows, :] = new.astype(BF16)
        for rows in spans:
            new = 1.25 * y_f[rows, :] - 0.25 * dot(z_b[rows, :], m_b[1])
            y_f[rows, :] = new
            y_b[rows, :] = new.astype(BF16)

    def sweep(_, carry):
        for side in range(2):
            for rows in spans:
                square = dot(m_b[side, rows, :], m_b[side])
                v_b[side, rows, :] = (0.0625 * square - 0.625 * m_f[side, rows, :]).astype(BF16)
        apply_factors()
        for side in range(2):
            for rows in spans:
                new = 1.5625 * m_f[side, rows, :] + dot(v_b[side, rows, :], m_b[side])
                w_f[side, rows, :] = new
                w_b[side, rows, :] = new.astype(BF16)
        for side in range(2):
            for rows in spans:
                new = 1.5625 * w_f[side, rows, :] + dot(v_b[side, rows, :], w_b[side])
                m_f[side, rows, :] = new
                m_b[side, rows, :] = new.astype(BF16)
        return carry

    lax.fori_loop(0, ITERS - 1, sweep, 0)
    apply_factors()
    norm_p = jnp.zeros((1, 1), F32)
    for rows in spans:
        new = y_f[rows, :] * scale
        norm_p += jnp.sum(new * new, keepdims=True)
        y_f[rows, :] = new
    ret_ref[...] = y_f[pl.ds(own, ROWS), :].astype(BF16)
    lane = lax.broadcasted_iota(jnp.int32, (N, LANES), 1)
    norms = jnp.zeros((N, LANES), F32)
    for k, part in enumerate(three_parts(norm_p) + three_parts(norm_g)):
        norms = jnp.where(lane == k, part, norms)
    norms = norms.astype(BF16)
    for zh in range(2):
        for row in range(N):
            rows = pl.ds(pl.multiple_of((zh * 4 + x) * ROWS + row * N, N), N)
            for k, ref in enumerate((y_f, base_f)):
                whole = ref[rows, :]
                half = jnp.where(co == 0, whole[:, :HALF], whole[:, HALF:])
                both = jnp.concatenate([half[:, :LANES], half[:, LANES:]], axis=0)
                msg_ref[zh * N + row, k * 2 * N : (k + 1) * 2 * N, :] = both.astype(BF16)
            msg_ref[zh * N + row, 4 * N : 5 * N, :] = norms


def weight_kernel(got_ref, ret_ref, mom_ref, half_ref, mom_out_ref, rows_f):
    total = jnp.zeros((N, LANES), F32)
    for z in range(4):
        for k in range(2 * N):
            total += got_ref[z, k, 4 * N : 5 * N, :].astype(F32)
    lane = lax.broadcasted_iota(jnp.int32, (N, LANES), 1)
    norm_p = jnp.sum(jnp.where(lane < 3, total, 0.0), keepdims=True) * (1.0 / N)
    norm_g = jnp.sum(jnp.where(lane < 3, 0.0, total), keepdims=True) * (1.0 / N)
    graft = jnp.sqrt(norm_g) / jnp.sqrt(norm_p)
    for j in range(N):
        slot = j % 2
        for zh in range(2):
            for z in range(4):
                i = zh * 4 + z
                precond = got_ref[z, zh * N + j, 0 : 2 * N, :].astype(F32)
                base = got_ref[z, zh * N + j, 2 * N : 4 * N, :].astype(F32)
                new = base - step_size * (graft * precond)
                for w in range(2):
                    rows_f[slot, w, i * N : (i + 1) * N, :] = new[w * N : (w + 1) * N, :]
        for p in range(N):
            for w in range(2):
                cols = slice(j * HALF + w * LANES, j * HALF + (w + 1) * LANES)
                half_ref[p, :, cols] = rows_f[slot, w, pl.ds(p, N, stride=N), :].astype(BF16)
    mom_out_ref[...] = moment_decay * mom_ref[...] + graft * ret_ref[...].astype(F32)


def join_kernel(got_ref, out_ref):
    for p in range(N):
        for j in range(N):
            for h in range(2):
                cols = slice(j * BLOCK + h * HALF, j * BLOCK + (h + 1) * HALF)
                out_ref[p, :, cols] = got_ref[h, p, :, j * HALF : (j + 1) * HALF]


def vmem(count):
    return [pl.BlockSpec(memory_space=pltpu.VMEM)] * count


def scratch(*shape, dtype):
    return pltpu.VMEM(shape, dtype)


def call(kernel, outs, scratches, flops=0, scalars=0, arrays=1, mib=32):
    return pl.pallas_call(
        kernel,
        out_shape=tuple(jax.ShapeDtypeStruct(*o) for o in outs),
        in_specs=[pl.BlockSpec(memory_space=pltpu.SMEM)] * scalars + vmem(arrays),
        out_specs=tuple(vmem(len(outs))),
        scratch_shapes=scratches,
        compiler_params=pltpu.CompilerParams(vmem_limit_bytes=mib * 1024 * 1024),
        cost_estimate=pl.CostEstimate(flops=flops, bytes_accessed=1 << 20, transcendentals=0),
    )


def step(gradients, left_stat, right_stat, momentum, master):
    own = (lax.axis_index("x") * 2 + lax.axis_index("co")).astype(jnp.int32).reshape(1)
    base = master[0] - (step_size * moment_decay) * momentum[0]
    share = jnp.concatenate([a.astype(BF16) for a in (left_stat[0], right_stat[0], base)], axis=0)
    s0 = turned(share)
    shares = [s0] + [along_x(s0, flip) for flip in (1, 2, 3)]
    twin = other_core(jnp.concatenate(shares, axis=0))

    (pieces,) = call(
        pack_kernel, [((N, 2 * ROWS, HALF), BF16)], [scratch(4, ROWS, LANES, dtype=F32)], mib=8
    )(gradients[0])
    pieces = exchanged(pieces, REP)
    mean = jnp.sum(pieces.astype(F32), axis=0) * (1.0 / N)
    mean = exchanged(mean.reshape(2 * N, N, HALF), PLANE)
    mean = spread(mean.reshape(2 * ROWS, HALF), "x")
    mean = spread(mean.reshape(BLOCK, HALF), "co")

    mean, grams, ret = call(
        gram_kernel,
        [((BLOCK, BLOCK), F32), ((2, BLOCK, BLOCK), F32), ((2 * ROWS, BLOCK), BF16)],
        [scratch(BLOCK, BLOCK, dtype=BF16)],
        flops=4 * BLOCK**3,
        scalars=1,
        mib=16,
    )(own, mean)
    ret = turned(ret)
    update = call(
        block_kernel,
        [((2 * N, MESSAGE, LANES), BF16), ((ROWS, BLOCK), BF16)],
        [
            scratch(2, BLOCK, BLOCK, dtype=F32),
            scratch(2, BLOCK, BLOCK, dtype=BF16),
            scratch(2, BLOCK, BLOCK, dtype=BF16),
            scratch(2, BLOCK, BLOCK, dtype=F32),
            scratch(2, BLOCK, BLOCK, dtype=BF16),
            scratch(BLOCK, BLOCK, dtype=F32),
            scratch(BLOCK, BLOCK, dtype=BF16),
            scratch(BLOCK, BLOCK, dtype=BF16),
            scratch(BLOCK, BLOCK, dtype=F32),
        ],
        flops=52 * BLOCK**3,
        scalars=1,
        arrays=7,
    )
    messages, rows = update(own, mean, grams, *shares, twin)
    rows = turned(rows)
    got = exchanged(messages, PLANE)
    got = spread(got, "zl")
    half, moment_rows = call(
        weight_kernel,
        [((N, N, N * HALF), BF16), ((ROWS, BLOCK), F32)],
        [scratch(2, 2, ROWS, LANES, dtype=F32)],
        arrays=3,
        mib=16,
    )(got, rows, momentum[0])
    half = spread(half, "co")
    (params,) = call(join_kernel, [((N, N, N * BLOCK), BF16)], [], mib=8)(half)
    left_next = stat_decay * left_stat[0] + (1.0 - stat_decay) * ret[:ROWS].astype(F32)
    right_next = stat_decay * right_stat[0] + (1.0 - stat_decay) * ret[ROWS:].astype(F32)
    return (params, moment_rows[None], left_next[None], right_next[None])


def solution(mesh):
    split = Mesh(mesh.devices.reshape(SIZES), ALL)
    in_specs = (P(REP, BLK, None, None),) + (P(BLK, REP, None),) * 4
    out_specs = (P(BLK, None, None),) + (P(BLK, REP, None),) * 3
    return jax.shard_map(step, mesh=split, in_specs=in_specs, out_specs=out_specs, check_vma=False)
```

time: 172 us -> 162 us (0.942)
  the two profiles are of different devices: /device:TPU:8 before, /device:TPU:13 now
where the time goes in v2:
time: 162 us
  blocking collectives  52 us (32%)
  waiting for transfers between devices  50.6 us (31%)
  starting transfers between devices  41.3 us (25%)
  Pallas kernels  13 us (8%)
  local copies, waits for them, and re-layouts  2.93 us (2%)
    all_to_all x4, blocking collectives, exchanged(): return lax.all_to_all(pieces, axis, split_axis=0, concat_axis=0, tiled=True)  52 us
    ppermute x7, waiting for transfers between devices, moved(): return lax.ppermute(shard, ALL, pairs)  45.5 us
    ppermute x7, starting transfers between devices, moved(): return lax.ppermute(shard, ALL, pairs)  23.5 us
    all_to_all x3, starting transfers between devices, exchanged(): return lax.all_to_all(pieces, axis, split_axis=0, concat_axis=0, tiled=True)  17.8 us
    pallas_call x1, Pallas kernels, step(): messages, rows = update(own, mean, grams, *shares, twin)  9.23 us
    all_to_all x3, waiting for transfers between devices, exchanged(): return lax.all_to_all(pieces, axis, split_axis=0, concat_axis=0, tiled=True)  5.09 us
  transfers between devices with their start and end apart: 10, of which 6 were waited for; matrix products, arithmetic and copies ran while one was open for 1% of the time, Pallas kernels for 0%

profile of v2, /device:TPU:13, one launch (start us, length us, event | category | flops | bytes accessed | tf_op | source)
XLA Modules:
  0.0 161.5 jit_solution(18051659610383649136)
XLA Ops:
  0.6 0.0 copy-start
  0.6 1.0 copy-done
  1.7 0.0 copy-start.1
  1.7 0.0 copy-start.4
  1.7 0.0 copy-start.2
  1.7 0.0 copy-start.3
  1.7 1.1 shard_map.84
  2.7 7.9 %all-to-all-start = ((bf16[8,128,256]{2,1,0:T(8,128)(2,1)}), bf16[8,128,256]{2,1,0:T(8,128)(2,1)S(1)}, u32[]{:S(2)}, u32[]{:S(2)}) async-start(bf16[8,128,256]{2,1,0:T(8,128)(2,1)} %shard_map.84), calls=%async_computation | async-start | bytes 1048576 | tf_op jit(solution)/shard_map/all_to_all | solution.py:33
  10.7 0.0 copy-done.1
  10.7 0.0 copy-done.4
  10.7 0.0 copy-done.2
  10.7 0.0 copy-done.3
  10.8 4.1 %collective-permute-start = (bf16[192,512]{1,0:T(8,128)(2,1)S(1)}, bf16[192,512]{1,0:T(8,128)(2,1)S(1)}, u32[]{:S(2)}, u32[]{:S(2)}) collective-permute-start(bf16[192,512]{1,0:T(8,128)(2,1)S(1)} %pad_maximum_fusion.1), channel_id=1, source_target_pairs={{0,0},{1,1},{2,2},{3,3},{4,4},{5,5},{6,6},{7,7},{8,128},{9,129},{1... | collective-permute-start | bytes 589832 | tf_op jit(solution)/shard_map/ppermute | solution.py:56
  14.9 18.6 %collective-permute-done.s0_ref = bf16[192,512]{1,0:T(8,128)(2,1)S(1)} collective-permute-done((bf16[192,512]{1,0:T(8,128)(2,1)S(1)}, bf16[192,512]{1,0:T(8,128)(2,1)S(1)}, u32[]{:S(2)}, u32[]{:S(2)}) %collective-permute-start) | collective-permute-done | bytes 196640 | tf_op jit(solution)/shard_map/ppermute | solution.py:56
  33.5 1.9 %collective-permute-start.1 = (bf16[192,512]{1,0:T(8,128)(2,1)S(1)}, bf16[192,512]{1,0:T(8,128)(2,1)S(1)}, u32[]{:S(2)}, u32[]{:S(2)}) collective-permute-start(bf16[192,512]{1,0:T(8,128)(2,1)S(1)} %collective-permute-done.s0_ref), channel_id=1, source_target_pairs={{0,8},{1,9},{2,10},{3,11},{4,12},{5,13},{6,14},{7,15},{8,0},{9,1},... | collective-permute-start | bytes 589832 | tf_op jit(solution)/shard_map/ppermute | solution.py:56
  35.5 1.9 %collective-permute-start.2 = (bf16[192,512]{1,0:T(8,128)(2,1)S(1)}, bf16[192,512]{1,0:T(8,128)(2,1)S(1)}, u32[]{:S(2)}, u32[]{:S(2)}) collective-permute-start(bf16[192,512]{1,0:T(8,128)(2,1)S(1)} %collective-permute-done.s0_ref), channel_id=1, source_target_pairs={{0,16},{1,17},{2,18},{3,19},{4,20},{5,21},{6,22},{7,23},{8,24},{9,... | collective-permute-start | bytes 589832 | tf_op jit(solution)/shard_map/ppermute | solution.py:56
  37.4 4.5 %collective-permute-start.3 = (bf16[192,512]{1,0:T(8,128)(2,1)S(1)}, bf16[192,512]{1,0:T(8,128)(2,1)S(1)}, u32[]{:S(2)}, u32[]{:S(2)}) collective-permute-start(bf16[192,512]{1,0:T(8,128)(2,1)S(1)} %collective-permute-done.s0_ref), channel_id=1, source_target_pairs={{0,24},{1,25},{2,26},{3,27},{4,28},{5,29},{6,30},{7,31},{8,16},{9,... | collective-permute-start | bytes 589832 | tf_op jit(solution)/shard_map/ppermute | solution.py:56
  41.9 0.0 collective-permute-done.1.s1_ref
  41.9 3.5 %collective-permute-done.2.s2_ref = bf16[192,512]{1,0:T(8,128)(2,1)S(1)} collective-permute-done((bf16[192,512]{1,0:T(8,128)(2,1)S(1)}, bf16[192,512]{1,0:T(8,128)(2,1)S(1)}, u32[]{:S(2)}, u32[]{:S(2)}) %collective-permute-start.2) | collective-permute-done | bytes 196640 | tf_op jit(solution)/shard_map/ppermute | solution.py:56
  45.4 5.0 %collective-permute-done.3.s3_ref = bf16[192,512]{1,0:T(8,128)(2,1)S(1)} collective-permute-done((bf16[192,512]{1,0:T(8,128)(2,1)S(1)}, bf16[192,512]{1,0:T(8,128)(2,1)S(1)}, u32[]{:S(2)}, u32[]{:S(2)}) %collective-permute-start.3) | collective-permute-done | bytes 196640 | tf_op jit(solution)/shard_map/ppermute | solution.py:56
  50.5 0.1 pad_maximum_fusion
  50.5 2.4 %collective-permute-start.4 = (bf16[768,512]{1,0:T(8,128)(2,1)S(1)}, bf16[768,512]{1,0:T(8,128)(2,1)S(1)}, u32[]{:S(2)}, u32[]{:S(2)}) collective-permute-start(bf16[768,512]{1,0:T(8,128)(2,1)S(1)} %pad_maximum_fusion), channel_id=1, source_target_pairs={{0,64},{1,65},{2,66},{3,67},{4,68},{5,69},{6,70},{7,71},{8,72},{9,... | collective-permute-start | bytes 2359304 | tf_op jit(solution)/shard_map/ppermute | solution.py:56
  52.9 0.0 all-to-all-done
  53.0 0.1 convert_reduce_fusion
  53.1 24.0 %all_to_all.35 = f32[16,8,256]{2,1,0:T(8,128)S(1)} all-to-all(f32[16,8,256]{2,1,0:T(8,128)S(1)} %multiply_bitcast_fusion), channel_id=1, replica_groups=mesh['zl'=4,'co'=2,'zh'=2,'x'=4,'y'=8] {'zh','y'}, dimensions={0} | all-to-all | bytes 262144 | tf_op jit(solution)/shard_map/all_to_all | solution.py:33
  77.1 0.8 broadcast_in_dim.36
  77.9 5.2 %all-to-all-start.2 = ((f32[4,128,256]{2,1,0:T(8,128)}), f32[4,128,256]{2,1,0:T(8,128)S(1)}, u32[]{:S(2)}, u32[]{:S(2)}) async-start(f32[4,128,256]{2,1,0:T(8,128)} %broadcast_in_dim.36), calls=%async_computation.2 | async-start | bytes 1048576 | tf_op jit(solution)/shard_map/all_to_all | solution.py:33
  83.1 5.1 %all-to-all-done.2 = f32[4,128,256]{2,1,0:T(8,128)S(1)} async-done(((f32[4,128,256]{2,1,0:T(8,128)}), f32[4,128,256]{2,1,0:T(8,128)S(1)}, u32[]{:S(2)}, u32[]{:S(2)}) %all-to-all-start.2) | async-done | bytes 524320 | tf_op jit(solution)/shard_map/all_to_all | solution.py:33
  88.2 0.1 broadcast_in_dim.38
  88.3 6.9 %all_to_all.36.got_ref = f32[2,512,256]{2,1,0:T(8,128)S(1)} all-to-all(f32[2,512,256]{2,1,0:T(8,128)S(1)} %broadcast_in_dim.38), channel_id=1, replica_groups=mesh['zl'=4,'co'=2,'zh'=2,'x'=4,'y'=8] {'co'}, dimensions={0} | all-to-all | bytes 2097152 | tf_op jit(solution)/shard_map/all_to_all | solution.py:33
  95.1 0.8 shard_map.85
  95.9 0.0 collective-permute-done.4.twin_ref
  96.0 9.2 %shard_map.86 = (bf16[16,40,128]{2,1,0:T(8,128)(2,1)S(1)}, bf16[64,512]{1,0:T(8,128)(2,1)S(1)}) custom-call(s32[1]{0:T(128)} %bitcast.own_ref, f32[512,512]{1,0:T(8,128)S(1)} %get-tuple-element.11.g_ref, f32[2,512,512]{2,1,0:T(8,128)S(1)} %get-tuple-element.12.gram_ref, bf16[192,512]{1,0:T(8,128)(2,1)S(1)} %collective-permute-done.s0_ref, ...), custom_call_target="tpu_custom_call" | custom-call | flops 6979321856 | bytes 1048576 | tf_op jit(solution)/shard_map/pallas_call | solution.py:304
  105.2 15.9 %all_to_all.37 = bf16[16,40,128]{2,1,0:T(8,128)(2,1)S(1)} all-to-all(bf16[16,40,128]{2,1,0:T(8,128)(2,1)S(1)} %get-tuple-element.13), channel_id=1, replica_groups=mesh['zl'=4,'co'=2,'zh'=2,'x'=4,'y'=8] {'zh','y'}, dimensions={0} | all-to-all | bytes 327680 | tf_op jit(solution)/shard_map/all_to_all | solution.py:33
  121.1 0.9 broadcast_in_dim.39
  122.0 4.7 %all-to-all-start.5 = ((bf16[4,16,40,128]{3,2,1,0:T(8,128)(2,1)}), bf16[4,16,40,128]{3,2,1,0:T(8,128)(2,1)S(1)}, u32[]{:S(2)}, u32[]{:S(2)}) async-start(bf16[4,16,40,128]{3,2,1,0:T(8,128)(2,1)} %broadcast_in_dim.39), calls=%async_computation.5 | async-start | bytes 1310720 | tf_op jit(solution)/shard_map/all_to_all | solution.py:33
  126.7 6.7 %collective-permute-start.6 = (bf16[128,512]{1,0:T(8,128)(2,1)S(1)}, bf16[128,512]{1,0:T(8,128)(2,1)S(1)}, u32[]{:S(2)}, u32[]{:S(2)}) collective-permute-start(bf16[128,512]{1,0:T(8,128)(2,1)S(1)} %get-tuple-element.17), channel_id=1, source_target_pairs={{0,0},{1,1},{2,2},{3,3},{4,4},{5,5},{6,6},{7,7},{8,128},{9,129},{1... | collective-permute-start | bytes 393224 | tf_op jit(solution)/shard_map/ppermute | solution.py:56
  133.4 1.9 %collective-permute-start.5 = (bf16[64,512]{1,0:T(8,128)(2,1)S(1)}, bf16[64,512]{1,0:T(8,128)(2,1)S(1)}, u32[]{:S(2)}, u32[]{:S(2)}) collective-permute-start(bf16[64,512]{1,0:T(8,128)(2,1)S(1)} %get-tuple-element.14), channel_id=1, source_target_pairs={{0,0},{1,1},{2,2},{3,3},{4,4},{5,5},{6,6},{7,7},{8,128},{9,129},{1... | collective-permute-start | bytes 196616 | tf_op jit(solution)/shard_map/ppermute | solution.py:56
  135.3 17.7 %collective-permute-done.6 = bf16[128,512]{1,0:T(8,128)(2,1)S(1)} collective-permute-done((bf16[128,512]{1,0:T(8,128)(2,1)S(1)}, bf16[128,512]{1,0:T(8,128)(2,1)S(1)}, u32[]{:S(2)}, u32[]{:S(2)}) %collective-permute-start.6) | collective-permute-done | bytes 131104 | tf_op jit(solution)/shard_map/ppermute | solution.py:56
  153.0 0.7 fusion
  153.7 0.7 collective-permute-done.5.ret_ref
  154.4 0.0 all-to-all-done.5.got_ref
  154.4 1.1 shard_map.87
  155.5 5.2 %all_to_all.38.got_ref = bf16[2,8,8,2048]{3,2,1,0:T(8,128)(2,1)S(1)} all-to-all(bf16[2,8,8,2048]{3,2,1,0:T(8,128)(2,1)S(1)} %broadcast_in_dim.40), channel_id=1, replica_groups=mesh['zl'=4,'co'=2,'zh'=2,'x'=4,'y'=8] {'co'}, dimensions={0} | all-to-all | bytes 1048576 | tf_op jit(solution)/shard_map/all_to_all | solution.py:33
  160.7 0.8 shard_map.88
  (5 shorter events, 0.1 us)
Async XLA Ops:
  0.6 1.0 copy-start
  1.7 9.0 %copy-start.1 = (f32[1,64,512]{2,1,0:T(8,128)S(1)}, f32[1,64,512]{2,1,0:T(8,128)}, u32[]{:S(2)}) copy-start(f32[1,64,512]{2,1,0:T(8,128)} %param.8) | copy-start | bytes 393220
  1.7 9.0 %copy-start.4 = (f32[1,64,512]{2,1,0:T(8,128)S(1)}, f32[1,64,512]{2,1,0:T(8,128)}, u32[]{:S(2)}) copy-start(f32[1,64,512]{2,1,0:T(8,128)} %param.9) | copy-start | bytes 393220
  1.7 9.0 %copy-start.2 = (f32[1,64,512]{2,1,0:T(8,128)S(1)}, f32[1,64,512]{2,1,0:T(8,128)}, u32[]{:S(2)}) copy-start(f32[1,64,512]{2,1,0:T(8,128)} %param.7) | copy-start | bytes 393220
  1.7 9.1 %copy-start.3 = (f32[1,64,512]{2,1,0:T(8,128)S(1)}, f32[1,64,512]{2,1,0:T(8,128)}, u32[]{:S(2)}) copy-start(f32[1,64,512]{2,1,0:T(8,128)} %param.6) | copy-start | bytes 393220
  2.7 50.2 %all-to-all-start = ((bf16[8,128,256]{2,1,0:T(8,128)(2,1)}), bf16[8,128,256]{2,1,0:T(8,128)(2,1)S(1)}, u32[]{:S(2)}, u32[]{:S(2)}) async-start(bf16[8,128,256]{2,1,0:T(8,128)(2,1)} %shard_map.84), calls=%async_computation | async-start | bytes 1048576 | tf_op jit(solution)/shard_map/all_to_all | solution.py:33
  10.8 22.8 %collective-permute-start = (bf16[192,512]{1,0:T(8,128)(2,1)S(1)}, bf16[192,512]{1,0:T(8,128)(2,1)S(1)}, u32[]{:S(2)}, u32[]{:S(2)}) collective-permute-start(bf16[192,512]{1,0:T(8,128)(2,1)S(1)} %pad_maximum_fusion.1), channel_id=1, source_target_pairs={{0,0},{1,1},{2,2},{3,3},{4,4},{5,5},{6,6},{7,7},{8,128},{9,129},{1... | collective-permute-start | bytes 589832 | tf_op jit(solution)/shard_map/ppermute | solution.py:56
  33.5 8.4 %collective-permute-start.1 = (bf16[192,512]{1,0:T(8,128)(2,1)S(1)}, bf16[192,512]{1,0:T(8,128)(2,1)S(1)}, u32[]{:S(2)}, u32[]{:S(2)}) collective-permute-start(bf16[192,512]{1,0:T(8,128)(2,1)S(1)} %collective-permute-done.s0_ref), channel_id=1, source_target_pairs={{0,8},{1,9},{2,10},{3,11},{4,12},{5,13},{6,14},{7,15},{8,0},{9,1},... | collective-permute-start | bytes 589832 | tf_op jit(solution)/shard_map/ppermute | solution.py:56
  35.5 10.0 %collective-permute-start.2 = (bf16[192,512]{1,0:T(8,128)(2,1)S(1)}, bf16[192,512]{1,0:T(8,128)(2,1)S(1)}, u32[]{:S(2)}, u32[]{:S(2)}) collective-permute-start(bf16[192,512]{1,0:T(8,128)(2,1)S(1)} %collective-permute-done.s0_ref), channel_id=1, source_target_pairs={{0,16},{1,17},{2,18},{3,19},{4,20},{5,21},{6,22},{7,23},{8,24},{9,... | collective-permute-start | bytes 589832 | tf_op jit(solution)/shard_map/ppermute | solution.py:56
  37.4 13.1 %collective-permute-start.3 = (bf16[192,512]{1,0:T(8,128)(2,1)S(1)}, bf16[192,512]{1,0:T(8,128)(2,1)S(1)}, u32[]{:S(2)}, u32[]{:S(2)}) collective-permute-start(bf16[192,512]{1,0:T(8,128)(2,1)S(1)} %collective-permute-done.s0_ref), channel_id=1, source_target_pairs={{0,24},{1,25},{2,26},{3,27},{4,28},{5,29},{6,30},{7,31},{8,16},{9,... | collective-permute-start | bytes 589832 | tf_op jit(solution)/shard_map/ppermute | solution.py:56
  50.5 45.4 %collective-permute-start.4 = (bf16[768,512]{1,0:T(8,128)(2,1)S(1)}, bf16[768,512]{1,0:T(8,128)(2,1)S(1)}, u32[]{:S(2)}, u32[]{:S(2)}) collective-permute-start(bf16[768,512]{1,0:T(8,128)(2,1)S(1)} %pad_maximum_fusion), channel_id=1, source_target_pairs={{0,64},{1,65},{2,66},{3,67},{4,68},{5,69},{6,70},{7,71},{8,72},{9,... | collective-permute-start | bytes 2359304 | tf_op jit(solution)/shard_map/ppermute | solution.py:56
  77.9 10.3 %all-to-all-start.2 = ((f32[4,128,256]{2,1,0:T(8,128)}), f32[4,128,256]{2,1,0:T(8,128)S(1)}, u32[]{:S(2)}, u32[]{:S(2)}) async-start(f32[4,128,256]{2,1,0:T(8,128)} %broadcast_in_dim.36), calls=%async_computation.2 | async-start | bytes 1048576 | tf_op jit(solution)/shard_map/all_to_all | solution.py:33
  122.0 32.4 %all-to-all-start.5 = ((bf16[4,16,40,128]{3,2,1,0:T(8,128)(2,1)}), bf16[4,16,40,128]{3,2,1,0:T(8,128)(2,1)S(1)}, u32[]{:S(2)}, u32[]{:S(2)}) async-start(bf16[4,16,40,128]{3,2,1,0:T(8,128)(2,1)} %broadcast_in_dim.39), calls=%async_computation.5 | async-start | bytes 1310720 | tf_op jit(solution)/shard_map/all_to_all | solution.py:33
  126.7 26.3 %collective-permute-start.6 = (bf16[128,512]{1,0:T(8,128)(2,1)S(1)}, bf16[128,512]{1,0:T(8,128)(2,1)S(1)}, u32[]{:S(2)}, u32[]{:S(2)}) collective-permute-start(bf16[128,512]{1,0:T(8,128)(2,1)S(1)} %get-tuple-element.17), channel_id=1, source_target_pairs={{0,0},{1,1},{2,2},{3,3},{4,4},{5,5},{6,6},{7,7},{8,128},{9,129},{1... | collective-permute-start | bytes 393224 | tf_op jit(solution)/shard_map/ppermute | solution.py:56
  133.4 21.0 %collective-permute-start.5 = (bf16[64,512]{1,0:T(8,128)(2,1)S(1)}, bf16[64,512]{1,0:T(8,128)(2,1)S(1)}, u32[]{:S(2)}, u32[]{:S(2)}) collective-permute-start(bf16[64,512]{1,0:T(8,128)(2,1)S(1)} %get-tuple-element.14), channel_id=1, source_target_pairs={{0,0},{1,1},{2,2},{3,3},{4,4},{5,5},{6,6},{7,7},{8,128},{9,129},{1... | collective-permute-start | bytes 196616 | tf_op jit(solution)/shard_map/ppermute | solution.py:56

commit v3 on v2

--- a/solution.py
+++ b/solution.py
@@ -10,6 +10,7 @@
 ALL = ("zl", "co", "zh", "x", "y")
 BLK = ("zh", "x", "y")
 PLANE = ("zh", "y")
+SOLID = ("zl", "zh", "y")
 SIZES = (4, 2, 2, 4, 8)
 N = 8
 ROWS = 64
@@ -199,15 +200,18 @@
                 whole = ref[rows, :]
                 half = jnp.where(co == 0, whole[:, :HALF], whole[:, HALF:])
                 both = jnp.concatenate([half[:, :LANES], half[:, LANES:]], axis=0)
-                msg_ref[zh * N + row, k * 2 * N : (k + 1) * 2 * N, :] = both.astype(BF16)
-            msg_ref[zh * N + row, 4 * N : 5 * N, :] = norms
+                both = both.astype(BF16)
+                for z in range(4):
+                    at = (z * 2 + zh) * N + row
+                    msg_ref[at, k * 2 * N : (k + 1) * 2 * N, :] = both
+            for z in range(4):
+                msg_ref[(z * 2 + zh) * N + row, 4 * N : 5 * N, :] = norms
 
 
 def weight_kernel(got_ref, ret_ref, mom_ref, half_ref, mom_out_ref, rows_f):
     total = jnp.zeros((N, LANES), F32)
-    for z in range(4):
-        for k in range(2 * N):
-            total += got_ref[z, k, 4 * N : 5 * N, :].astype(F32)
+    for k in range(8 * N):
+        total += got_ref[k, 4 * N : 5 * N, :].astype(F32)
     lane = lax.broadcasted_iota(jnp.int32, (N, LANES), 1)
     norm_p = jnp.sum(jnp.where(lane < 3, total, 0.0), keepdims=True) * (1.0 / N)
     norm_g = jnp.sum(jnp.where(lane < 3, 0.0, total), keepdims=True) * (1.0 / N)
@@ -217,8 +221,9 @@
         for zh in range(2):
             for z in range(4):
                 i = zh * 4 + z
-                precond = got_ref[z, zh * N + j, 0 : 2 * N, :].astype(F32)
-                base = got_ref[z, zh * N + j, 2 * N : 4 * N, :].astype(F32)
+                at = (z * 2 + zh) * N + j
+                precond = got_ref[at, 0 : 2 * N, :].astype(F32)
+                base = got_ref[at, 2 * N : 4 * N, :].astype(F32)
                 new = base - step_size * (graft * precond)
                 for w in range(2):
                     rows_f[slot, w, i * N : (i + 1) * N, :] = new[w * N : (w + 1) * N, :]
@@ -285,7 +290,7 @@
     ret = turned(ret)
     update = call(
         block_kernel,
-        [((2 * N, MESSAGE, LANES), BF16), ((ROWS, BLOCK), BF16)],
+        [((8 * N, MESSAGE, LANES), BF16), ((ROWS, BLOCK), BF16)],
         [
             scratch(2, BLOCK, BLOCK, dtype=F32),
             scratch(2, BLOCK, BLOCK, dtype=BF16),
@@ -303,8 +308,7 @@
     )
     messages, rows = update(own, mean, grams, *shares, twin)
     rows = turned(rows)
-    got = exchanged(messages, PLANE)
-    got = spread(got, "zl")
+    got = exchanged(messages, SOLID)
     half, moment_rows = call(
         weight_kernel,
         [((N, N, N * HALF), BF16), ((ROWS, BLOCK), F32)],

time: 162 us -> 153 us (0.944)
  the two profiles are of different devices: /device:TPU:13 before, /device:TPU:27 now
where the time goes in v3:
time: 153 us; the launch traced here: 152 us
  waiting for transfers between devices  51.3 us (34%)
  starting transfers between devices  49.6 us (32%)
  blocking collectives  33.4 us (22%)
  Pallas kernels  13.8 us (9%)
  local copies, waits for them, and re-layouts  2 us (1%)
    ppermute x7, waiting for transfers between devices, moved(): return lax.ppermute(shard, ALL, pairs)  44.4 us
    all_to_all x3, blocking collectives, exchanged(): return lax.all_to_all(pieces, axis, split_axis=0, concat_axis=0, tiled=True)  33.4 us
    ppermute x7, starting transfers between devices, moved(): return lax.ppermute(shard, ALL, pairs)  28.7 us
    all_to_all x3, starting transfers between devices, exchanged(): return lax.all_to_all(pieces, axis, split_axis=0, concat_axis=0, tiled=True)  20.9 us
    pallas_call x1, Pallas kernels, step(): messages, rows = update(own, mean, grams, *shares, twin)  10.1 us
    all_to_all x3, waiting for transfers between devices, exchanged(): return lax.all_to_all(pieces, axis, split_axis=0, concat_axis=0, tiled=True)  6.89 us
  transfers between devices with their start and end apart: 10, of which 6 were waited for; matrix products, arithmetic and copies ran while one was open for 1% of the time, Pallas kernels for 1%

profile of v3, /device:TPU:27, one launch (start us, length us, event | category | flops | bytes accessed | tf_op | source)
XLA Modules:
  0.0 151.9 jit_solution(9977427640408499611)
XLA Ops:
  0.6 0.0 copy-start
  0.6 1.0 copy-done
  1.7 0.0 copy-start.1
  1.7 0.0 copy-start.4
  1.7 0.0 copy-start.2
  1.7 0.0 copy-start.3
  1.7 1.1 shard_map.84
  2.7 7.9 %all-to-all-start = ((bf16[8,128,256]{2,1,0:T(8,128)(2,1)}), bf16[8,128,256]{2,1,0:T(8,128)(2,1)S(1)}, u32[]{:S(2)}, u32[]{:S(2)}) async-start(bf16[8,128,256]{2,1,0:T(8,128)(2,1)} %shard_map.84), calls=%async_computation | async-start | bytes 1048576 | tf_op jit(solution)/shard_map/all_to_all | solution.py:34
  10.7 0.0 copy-done.1
  10.7 0.0 copy-done.4
  10.7 0.0 copy-done.2
  10.7 0.0 copy-done.3
  10.8 3.2 %collective-permute-start = (bf16[192,512]{1,0:T(8,128)(2,1)S(1)}, bf16[192,512]{1,0:T(8,128)(2,1)S(1)}, u32[]{:S(2)}, u32[]{:S(2)}) collective-permute-start(bf16[192,512]{1,0:T(8,128)(2,1)S(1)} %pad_maximum_fusion.1), channel_id=1, source_target_pairs={{0,0},{1,1},{2,2},{3,3},{4,4},{5,5},{6,6},{7,7},{8,128},{9,129},{1... | collective-permute-start | bytes 589832 | tf_op jit(solution)/shard_map/ppermute | solution.py:57
  14.0 11.0 %collective-permute-done.s0_ref = bf16[192,512]{1,0:T(8,128)(2,1)S(1)} collective-permute-done((bf16[192,512]{1,0:T(8,128)(2,1)S(1)}, bf16[192,512]{1,0:T(8,128)(2,1)S(1)}, u32[]{:S(2)}, u32[]{:S(2)}) %collective-permute-start) | collective-permute-done | bytes 196640 | tf_op jit(solution)/shard_map/ppermute | solution.py:57
  25.0 1.9 %collective-permute-start.1 = (bf16[192,512]{1,0:T(8,128)(2,1)S(1)}, bf16[192,512]{1,0:T(8,128)(2,1)S(1)}, u32[]{:S(2)}, u32[]{:S(2)}) collective-permute-start(bf16[192,512]{1,0:T(8,128)(2,1)S(1)} %collective-permute-done.s0_ref), channel_id=1, source_target_pairs={{0,8},{1,9},{2,10},{3,11},{4,12},{5,13},{6,14},{7,15},{8,0},{9,1},... | collective-permute-start | bytes 589832 | tf_op jit(solution)/shard_map/ppermute | solution.py:57
  26.9 12.8 %collective-permute-start.2 = (bf16[192,512]{1,0:T(8,128)(2,1)S(1)}, bf16[192,512]{1,0:T(8,128)(2,1)S(1)}, u32[]{:S(2)}, u32[]{:S(2)}) collective-permute-start(bf16[192,512]{1,0:T(8,128)(2,1)S(1)} %collective-permute-done.s0_ref), channel_id=1, source_target_pairs={{0,16},{1,17},{2,18},{3,19},{4,20},{5,21},{6,22},{7,23},{8,24},{9,... | collective-permute-start | bytes 589832 | tf_op jit(solution)/shard_map/ppermute | solution.py:57
  39.8 1.9 %collective-permute-start.3 = (bf16[192,512]{1,0:T(8,128)(2,1)S(1)}, bf16[192,512]{1,0:T(8,128)(2,1)S(1)}, u32[]{:S(2)}, u32[]{:S(2)}) collective-permute-start(bf16[192,512]{1,0:T(8,128)(2,1)S(1)} %collective-permute-done.s0_ref), channel_id=1, source_target_pairs={{0,24},{1,25},{2,26},{3,27},{4,28},{5,29},{6,30},{7,31},{8,16},{9,... | collective-permute-start | bytes 589832 | tf_op jit(solution)/shard_map/ppermute | solution.py:57
  41.7 0.0 collective-permute-done.1.s1_ref
  41.7 4.3 %collective-permute-done.2.s2_ref = bf16[192,512]{1,0:T(8,128)(2,1)S(1)} collective-permute-done((bf16[192,512]{1,0:T(8,128)(2,1)S(1)}, bf16[192,512]{1,0:T(8,128)(2,1)S(1)}, u32[]{:S(2)}, u32[]{:S(2)}) %collective-permute-start.2) | collective-permute-done | bytes 196640 | tf_op jit(solution)/shard_map/ppermute | solution.py:57
  46.0 5.2 %collective-permute-done.3.s3_ref = bf16[192,512]{1,0:T(8,128)(2,1)S(1)} collective-permute-done((bf16[192,512]{1,0:T(8,128)(2,1)S(1)}, bf16[192,512]{1,0:T(8,128)(2,1)S(1)}, u32[]{:S(2)}, u32[]{:S(2)}) %collective-permute-start.3) | collective-permute-done | bytes 196640 | tf_op jit(solution)/shard_map/ppermute | solution.py:57
  51.1 0.1 pad_maximum_fusion
  51.2 2.6 %collective-permute-start.4 = (bf16[768,512]{1,0:T(8,128)(2,1)S(1)}, bf16[768,512]{1,0:T(8,128)(2,1)S(1)}, u32[]{:S(2)}, u32[]{:S(2)}) collective-permute-start(bf16[768,512]{1,0:T(8,128)(2,1)S(1)} %pad_maximum_fusion), channel_id=1, source_target_pairs={{0,64},{1,65},{2,66},{3,67},{4,68},{5,69},{6,70},{7,71},{8,72},{9,... | collective-permute-start | bytes 2359304 | tf_op jit(solution)/shard_map/ppermute | solution.py:57
  53.8 0.0 all-to-all-done
  53.8 0.1 convert_reduce_fusion
  53.9 22.6 %all_to_all.30 = f32[16,8,256]{2,1,0:T(8,128)S(1)} all-to-all(f32[16,8,256]{2,1,0:T(8,128)S(1)} %multiply_bitcast_fusion), channel_id=1, replica_groups=mesh['zl'=4,'co'=2,'zh'=2,'x'=4,'y'=8] {'zh','y'}, dimensions={0} | all-to-all | bytes 262144 | tf_op jit(solution)/shard_map/all_to_all | solution.py:34
  76.5 0.8 broadcast_in_dim.30
  77.4 4.3 %all-to-all-start.2 = ((f32[4,128,256]{2,1,0:T(8,128)}), f32[4,128,256]{2,1,0:T(8,128)S(1)}, u32[]{:S(2)}, u32[]{:S(2)}) async-start(f32[4,128,256]{2,1,0:T(8,128)} %broadcast_in_dim.30), calls=%async_computation.2 | async-start | bytes 1048576 | tf_op jit(solution)/shard_map/all_to_all | solution.py:34
  81.7 6.9 %all-to-all-done.2 = f32[4,128,256]{2,1,0:T(8,128)S(1)} async-done(((f32[4,128,256]{2,1,0:T(8,128)}), f32[4,128,256]{2,1,0:T(8,128)S(1)}, u32[]{:S(2)}, u32[]{:S(2)}) %all-to-all-start.2) | async-done | bytes 524320 | tf_op jit(solution)/shard_map/all_to_all | solution.py:34
  88.6 0.1 broadcast_in_dim.32
  88.7 6.6 %all_to_all.31.got_ref = f32[2,512,256]{2,1,0:T(8,128)S(1)} all-to-all(f32[2,512,256]{2,1,0:T(8,128)S(1)} %broadcast_in_dim.32), channel_id=1, replica_groups=mesh['zl'=4,'co'=2,'zh'=2,'x'=4,'y'=8] {'co'}, dimensions={0} | all-to-all | bytes 2097152 | tf_op jit(solution)/shard_map/all_to_all | solution.py:34
  95.3 0.8 shard_map.85
  96.1 0.0 collective-permute-done.4.twin_ref
  96.1 10.1 %shard_map.86 = (bf16[64,40,128]{2,1,0:T(8,128)(2,1)}, bf16[64,512]{1,0:T(8,128)(2,1)S(1)}) custom-call(s32[1]{0:T(128)} %bitcast.own_ref, f32[512,512]{1,0:T(8,128)S(1)} %get-tuple-element.11.g_ref, f32[2,512,512]{2,1,0:T(8,128)S(1)} %get-tuple-element.12.gram_ref, bf16[192,512]{1,0:T(8,128)(2,1)S(1)} %collective-permute-done.s0_ref, ...), custom_call_target="tpu_custom_call" | custom-call | flops 6979321856 | bytes 1048576 | tf_op jit(solution)/shard_map/pallas_call | solution.py:309
  106.2 8.7 %all-to-all-start.4 = ((bf16[64,40,128]{2,1,0:T(8,128)(2,1)}), bf16[64,40,128]{2,1,0:T(8,128)(2,1)S(1)}, u32[]{:S(2)}, u32[]{:S(2)}) async-start(bf16[64,40,128]{2,1,0:T(8,128)(2,1)} %get-tuple-element.13), calls=%async_computation.4 | async-start | bytes 1310720 | tf_op jit(solution)/shard_map/all_to_all | solution.py:34
  114.8 4.0 %collective-permute-start.6 = (bf16[128,512]{1,0:T(8,128)(2,1)S(1)}, bf16[128,512]{1,0:T(8,128)(2,1)S(1)}, u32[]{:S(2)}, u32[]{:S(2)}) collective-permute-start(bf16[128,512]{1,0:T(8,128)(2,1)S(1)} %get-tuple-element.17), channel_id=1, source_target_pairs={{0,0},{1,1},{2,2},{3,3},{4,4},{5,5},{6,6},{7,7},{8,128},{9,129},{1... | collective-permute-start | bytes 393224 | tf_op jit(solution)/shard_map/ppermute | solution.py:57
  118.8 2.2 %collective-permute-start.5 = (bf16[64,512]{1,0:T(8,128)(2,1)S(1)}, bf16[64,512]{1,0:T(8,128)(2,1)S(1)}, u32[]{:S(2)}, u32[]{:S(2)}) collective-permute-start(bf16[64,512]{1,0:T(8,128)(2,1)S(1)} %get-tuple-element.14), channel_id=1, source_target_pairs={{0,0},{1,1},{2,2},{3,3},{4,4},{5,5},{6,6},{7,7},{8,128},{9,129},{1... | collective-permute-start | bytes 196616 | tf_op jit(solution)/shard_map/ppermute | solution.py:57
  121.0 23.3 %collective-permute-done.6 = bf16[128,512]{1,0:T(8,128)(2,1)S(1)} collective-permute-done((bf16[128,512]{1,0:T(8,128)(2,1)S(1)}, bf16[128,512]{1,0:T(8,128)(2,1)S(1)}, u32[]{:S(2)}, u32[]{:S(2)}) %collective-permute-start.6) | collective-permute-done | bytes 131104 | tf_op jit(solution)/shard_map/ppermute | solution.py:57
  144.3 0.7 fusion
  145.0 0.7 collective-permute-done.5.ret_ref
  145.7 0.0 all-to-all-done.4.got_ref
  145.7 1.1 shard_map.87
  146.8 4.3 %all_to_all.32.got_ref = bf16[2,8,8,2048]{3,2,1,0:T(8,128)(2,1)S(1)} all-to-all(bf16[2,8,8,2048]{3,2,1,0:T(8,128)(2,1)S(1)} %broadcast_in_dim.33), channel_id=1, replica_groups=mesh['zl'=4,'co'=2,'zh'=2,'x'=4,'y'=8] {'co'}, dimensions={0} | all-to-all | bytes 1048576 | tf_op jit(solution)/shard_map/all_to_all | solution.py:34
  151.1 0.8 shard_map.88
  (5 shorter events, 0.1 us)
Async XLA Ops:
  0.6 1.0 copy-start
  1.7 9.0 %copy-start.1 = (f32[1,64,512]{2,1,0:T(8,128)S(1)}, f32[1,64,512]{2,1,0:T(8,128)}, u32[]{:S(2)}) copy-start(f32[1,64,512]{2,1,0:T(8,128)} %param.8) | copy-start | bytes 393220
  1.7 9.0 %copy-start.4 = (f32[1,64,512]{2,1,0:T(8,128)S(1)}, f32[1,64,512]{2,1,0:T(8,128)}, u32[]{:S(2)}) copy-start(f32[1,64,512]{2,1,0:T(8,128)} %param.9) | copy-start | bytes 393220
  1.7 9.0 %copy-start.2 = (f32[1,64,512]{2,1,0:T(8,128)S(1)}, f32[1,64,512]{2,1,0:T(8,128)}, u32[]{:S(2)}) copy-start(f32[1,64,512]{2,1,0:T(8,128)} %param.7) | copy-start | bytes 393220
  1.7 9.1 %copy-start.3 = (f32[1,64,512]{2,1,0:T(8,128)S(1)}, f32[1,64,512]{2,1,0:T(8,128)}, u32[]{:S(2)}) copy-start(f32[1,64,512]{2,1,0:T(8,128)} %param.6) | copy-start | bytes 393220
  2.7 51.1 %all-to-all-start = ((bf16[8,128,256]{2,1,0:T(8,128)(2,1)}), bf16[8,128,256]{2,1,0:T(8,128)(2,1)S(1)}, u32[]{:S(2)}, u32[]{:S(2)}) async-start(bf16[8,128,256]{2,1,0:T(8,128)(2,1)} %shard_map.84), calls=%async_computation | async-start | bytes 1048576 | tf_op jit(solution)/shard_map/all_to_all | solution.py:34
  10.8 14.2 %collective-permute-start = (bf16[192,512]{1,0:T(8,128)(2,1)S(1)}, bf16[192,512]{1,0:T(8,128)(2,1)S(1)}, u32[]{:S(2)}, u32[]{:S(2)}) collective-permute-start(bf16[192,512]{1,0:T(8,128)(2,1)S(1)} %pad_maximum_fusion.1), channel_id=1, source_target_pairs={{0,0},{1,1},{2,2},{3,3},{4,4},{5,5},{6,6},{7,7},{8,128},{9,129},{1... | collective-permute-start | bytes 589832 | tf_op jit(solution)/shard_map/ppermute | solution.py:57
  25.0 16.7 %collective-permute-start.1 = (bf16[192,512]{1,0:T(8,128)(2,1)S(1)}, bf16[192,512]{1,0:T(8,128)(2,1)S(1)}, u32[]{:S(2)}, u32[]{:S(2)}) collective-permute-start(bf16[192,512]{1,0:T(8,128)(2,1)S(1)} %collective-permute-done.s0_ref), channel_id=1, source_target_pairs={{0,8},{1,9},{2,10},{3,11},{4,12},{5,13},{6,14},{7,15},{8,0},{9,1},... | collective-permute-start | bytes 589832 | tf_op jit(solution)/shard_map/ppermute | solution.py:57
  26.9 19.0 %collective-permute-start.2 = (bf16[192,512]{1,0:T(8,128)(2,1)S(1)}, bf16[192,512]{1,0:T(8,128)(2,1)S(1)}, u32[]{:S(2)}, u32[]{:S(2)}) collective-permute-start(bf16[192,512]{1,0:T(8,128)(2,1)S(1)} %collective-permute-done.s0_ref), channel_id=1, source_target_pairs={{0,16},{1,17},{2,18},{3,19},{4,20},{5,21},{6,22},{7,23},{8,24},{9,... | collective-permute-start | bytes 589832 | tf_op jit(solution)/shard_map/ppermute | solution.py:57
  39.8 11.4 %collective-permute-start.3 = (bf16[192,512]{1,0:T(8,128)(2,1)S(1)}, bf16[192,512]{1,0:T(8,128)(2,1)S(1)}, u32[]{:S(2)}, u32[]{:S(2)}) collective-permute-start(bf16[192,512]{1,0:T(8,128)(2,1)S(1)} %collective-permute-done.s0_ref), channel_id=1, source_target_pairs={{0,24},{1,25},{2,26},{3,27},{4,28},{5,29},{6,30},{7,31},{8,16},{9,... | collective-permute-start | bytes 589832 | tf_op jit(solution)/shard_map/ppermute | solution.py:57
  51.2 44.9 %collective-permute-start.4 = (bf16[768,512]{1,0:T(8,128)(2,1)S(1)}, bf16[768,512]{1,0:T(8,128)(2,1)S(1)}, u32[]{:S(2)}, u32[]{:S(2)}) collective-permute-start(bf16[768,512]{1,0:T(8,128)(2,1)S(1)} %pad_maximum_fusion), channel_id=1, source_target_pairs={{0,64},{1,65},{2,66},{3,67},{4,68},{5,69},{6,70},{7,71},{8,72},{9,... | collective-permute-start | bytes 2359304 | tf_op jit(solution)/shard_map/ppermute | solution.py:57
  77.4 11.2 %all-to-all-start.2 = ((f32[4,128,256]{2,1,0:T(8,128)}), f32[4,128,256]{2,1,0:T(8,128)S(1)}, u32[]{:S(2)}, u32[]{:S(2)}) async-start(f32[4,128,256]{2,1,0:T(8,128)} %broadcast_in_dim.30), calls=%async_computation.2 | async-start | bytes 1048576 | tf_op jit(solution)/shard_map/all_to_all | solution.py:34
  106.2 39.6 %all-to-all-start.4 = ((bf16[64,40,128]{2,1,0:T(8,128)(2,1)}), bf16[64,40,128]{2,1,0:T(8,128)(2,1)S(1)}, u32[]{:S(2)}, u32[]{:S(2)}) async-start(bf16[64,40,128]{2,1,0:T(8,128)(2,1)} %get-tuple-element.13), calls=%async_computation.4 | async-start | bytes 1310720 | tf_op jit(solution)/shard_map/all_to_all | solution.py:34
  114.8 29.5 %collective-permute-start.6 = (bf16[128,512]{1,0:T(8,128)(2,1)S(1)}, bf16[128,512]{1,0:T(8,128)(2,1)S(1)}, u32[]{:S(2)}, u32[]{:S(2)}) collective-permute-start(bf16[128,512]{1,0:T(8,128)(2,1)S(1)} %get-tuple-element.17), channel_id=1, source_target_pairs={{0,0},{1,1},{2,2},{3,3},{4,4},{5,5},{6,6},{7,7},{8,128},{9,129},{1... | collective-permute-start | bytes 393224 | tf_op jit(solution)/shard_map/ppermute | solution.py:57
  118.8 26.9 %collective-permute-start.5 = (bf16[64,512]{1,0:T(8,128)(2,1)S(1)}, bf16[64,512]{1,0:T(8,128)(2,1)S(1)}, u32[]{:S(2)}, u32[]{:S(2)}) collective-permute-start(bf16[64,512]{1,0:T(8,128)(2,1)S(1)} %get-tuple-element.14), channel_id=1, source_target_pairs={{0,0},{1,1},{2,2},{3,3},{4,4},{5,5},{6,6},{7,7},{8,128},{9,129},{1... | collective-permute-start | bytes 196616 | tf_op jit(solution)/shard_map/ppermute | solution.py:57

commit v4 on v3

--- a/solution.py
+++ b/solution.py
@@ -85,8 +85,23 @@
     return lax.dot_general(a, b, (dims, ((), ())), preferred_element_type=F32)
 
 
-def pack_kernel(grad_ref, out_ref, rows_f):
+def pack_kernel(
+    grad_hbm, left_hbm, right_hbm, mom_hbm, master_hbm,
+    out_ref, share_ref, grad_ref, rows_f, state_f, grad_sem, state_sem,
+):
+    loads = []
     for j in range(N):
+        cols = pl.ds(j * BLOCK, BLOCK)
+        load = pltpu.make_async_copy(grad_hbm.at[:, :, cols], grad_ref.at[:, :, cols], grad_sem.at[j])
+        load.start()
+        loads.append(load)
+    states = []
+    for k, ref in enumerate((left_hbm, right_hbm, mom_hbm, master_hbm)):
+        load = pltpu.make_async_copy(ref, state_f.at[k], state_sem.at[k])
+        load.start()
+        states.append(load)
+    for j in range(N):
+        loads[j].wait()
         for w in range(WIDE):
             slot = (j * WIDE + w) % 4
             for p in range(N):
@@ -97,6 +112,12 @@
                 at = (i // 4 * N + j) * N
                 rows = rows_f[slot, pl.ds(i, N, stride=N), :]
                 out_ref[i % 4 * 2 + w // 2, at : at + N, lanes] = rows.astype(BF16)
+    for load in states:
+        load.wait()
+    share_ref[0:ROWS, :] = state_f[0].astype(BF16)
+    share_ref[ROWS : 2 * ROWS, :] = state_f[1].astype(BF16)
+    base = state_f[3] - (step_size * moment_decay) * state_f[2]
+    share_ref[2 * ROWS : 3 * ROWS, :] = base.astype(BF16)
 
 
 def gram_kernel(own_ref, got_ref, g_ref, gram_ref, ret_ref, g_b):
@@ -208,7 +229,7 @@
                 msg_ref[(z * 2 + zh) * N + row, 4 * N : 5 * N, :] = norms
 
 
-def weight_kernel(got_ref, ret_ref, mom_ref, half_ref, mom_out_ref, rows_f):
+def weight_kernel(got_ref, half_ref, graft_ref, rows_f):
     total = jnp.zeros((N, LANES), F32)
     for k in range(8 * N):
         total += got_ref[k, 4 * N : 5 * N, :].astype(F32)
@@ -231,7 +252,7 @@
             for w in range(2):
                 cols = slice(j * HALF + w * LANES, j * HALF + (w + 1) * LANES)
                 half_ref[p, :, cols] = rows_f[slot, w, pl.ds(p, N, stride=N), :].astype(BF16)
-    mom_out_ref[...] = moment_decay * mom_ref[...] + graft * ret_ref[...].astype(F32)
+    graft_ref[...] = jnp.broadcast_to(graft, (N, LANES))
 
 
 def join_kernel(got_ref, out_ref):
@@ -250,11 +271,12 @@
     return pltpu.VMEM(shape, dtype)
 
 
-def call(kernel, outs, scratches, flops=0, scalars=0, arrays=1, mib=32):
+def call(kernel, outs, scratches, flops=0, scalars=0, arrays=1, mib=32, space=pltpu.VMEM):
     return pl.pallas_call(
         kernel,
         out_shape=tuple(jax.ShapeDtypeStruct(*o) for o in outs),
-        in_specs=[pl.BlockSpec(memory_space=pltpu.SMEM)] * scalars + vmem(arrays),
+        in_specs=[pl.BlockSpec(memory_space=pltpu.SMEM)] * scalars
+        + [pl.BlockSpec(memory_space=space)] * arrays,
         out_specs=tuple(vmem(len(outs))),
         scratch_shapes=scratches,
         compiler_params=pltpu.CompilerParams(vmem_limit_bytes=mib * 1024 * 1024),
@@ -264,15 +286,24 @@
 
 def step(gradients, left_stat, right_stat, momentum, master):
     own = (lax.axis_index("x") * 2 + lax.axis_index("co")).astype(jnp.int32).reshape(1)
-    base = master[0] - (step_size * moment_decay) * momentum[0]
-    share = jnp.concatenate([a.astype(BF16) for a in (left_stat[0], right_stat[0], base)], axis=0)
+    pieces, share = call(
+        pack_kernel,
+        [((N, 2 * ROWS, HALF), BF16), ((SHARE, BLOCK), BF16)],
+        [
+            scratch(N, N, N * BLOCK, dtype=BF16),
+            scratch(4, ROWS, LANES, dtype=F32),
+            scratch(4, ROWS, BLOCK, dtype=F32),
+            pltpu.SemaphoreType.DMA((N,)),
+            pltpu.SemaphoreType.DMA((4,)),
+        ],
+        arrays=5,
+        mib=60,
+        space=pltpu.HBM,
+    )(gradients[0], left_stat[0], right_stat[0], momentum[0], master[0])
     s0 = turned(share)
     shares = [s0] + [along_x(s0, flip) for flip in (1, 2, 3)]
     twin = other_core(jnp.concatenate(shares, axis=0))
 
-    (pieces,) = call(
-        pack_kernel, [((N, 2 * ROWS, HALF), BF16)], [scratch(4, ROWS, LANES, dtype=F32)], mib=8
-    )(gradients[0])
     pieces = exchanged(pieces, REP)
     mean = jnp.sum(pieces.astype(F32), axis=0) * (1.0 / N)
     mean = exchanged(mean.reshape(2 * N, N, HALF), PLANE)
@@ -308,16 +339,18 @@
     )
     messages, rows = update(own, mean, grams, *shares, twin)
     rows = turned(rows)
+    messages, ret = lax.optimization_barrier((messages, ret))
     got = exchanged(messages, SOLID)
-    half, moment_rows = call(
+    ret, got = lax.optimization_barrier((ret, got))
+    half, graft = call(
         weight_kernel,
-        [((N, N, N * HALF), BF16), ((ROWS, BLOCK), F32)],
+        [((N, N, N * HALF), BF16), ((N, LANES), F32)],
         [scratch(2, 2, ROWS, LANES, dtype=F32)],
-        arrays=3,
         mib=16,
-    )(got, rows, momentum[0])
+    )(got)
     half = spread(half, "co")
     (params,) = call(join_kernel, [((N, N, N * BLOCK), BF16)], [], mib=8)(half)
+    moment_rows = moment_decay * momentum[0] + graft[0, 0] * rows.astype(F32)
     left_next = stat_decay * left_stat[0] + (1.0 - stat_decay) * ret[:ROWS].astype(F32)
     right_next = stat_decay * right_stat[0] + (1.0 - stat_decay) * ret[ROWS:].astype(F32)
     return (params, moment_rows[None], left_next[None], right_next[None])

time: 153 us -> 150 us (0.980)
  the two profiles are of different devices: /device:TPU:27 before, /device:TPU:1 now
where the time goes in v4:
time: 150 us; the launch traced here: 149 us
  starting transfers between devices  65.5 us (44%)
  waiting for transfers between devices  35.1 us (23%)
  blocking collectives  29.3 us (20%)
  Pallas kernels  14.3 us (10%)
  local copies, waits for them, and re-layouts  2.28 us (2%)
  other arithmetic  2.11 us (1%)
    ppermute x7, starting transfers between devices, moved(): return lax.ppermute(shard, ALL, pairs)  35.5 us
    all_to_all x4, starting transfers between devices, exchanged(): return lax.all_to_all(pieces, axis, split_axis=0, concat_axis=0, tiled=True)  30 us
    all_to_all x2, blocking collectives, exchanged(): return lax.all_to_all(pieces, axis, split_axis=0, concat_axis=0, tiled=True)  29.3 us
    all_to_all x4, waiting for transfers between devices, exchanged(): return lax.all_to_all(pieces, axis, split_axis=0, concat_axis=0, tiled=True)  25.5 us
    pallas_call x1, Pallas kernels, step(): messages, rows = update(own, mean, grams, *shares, twin)  10.1 us
    ppermute x7, waiting for transfers between devices, moved(): return lax.ppermute(shard, ALL, pairs)  9.65 us
  transfers between devices with their start and end apart: 11, of which 5 were waited for; matrix products, arithmetic and copies ran while one was open for 2% of the time, Pallas kernels for 8%

profile of v4, /device:TPU:1, one launch (start us, length us, event | category | flops | bytes accessed | tf_op | source)
XLA Modules:
  0.0 149.3 jit_solution(13155164522525865929)
XLA Ops:
  0.6 2.2 %shard_map.84 = (bf16[8,128,256]{2,1,0:T(8,128)(2,1)}, bf16[192,512]{1,0:T(8,128)(2,1)}) custom-call(bf16[8,8,4096]{2,1,0:T(8,128)(2,1)} %bitcast.22, f32[64,512]{1,0:T(8,128)} %bitcast.23, f32[64,512]{1,0:T(8,128)} %bitcast.24, f32[64,512]{1,0:T(8,128)} %bitcast.25, f32[64,512]{1,0:T(8,128)} %bitcast.26), custom_call_target="tpu_custom_call" | custom-call | bytes 1048576 | tf_op jit(solution)/shard_map/pallas_call | solution.py:289
  2.9 10.2 %all-to-all-start = ((bf16[8,128,256]{2,1,0:T(8,128)(2,1)}), bf16[8,128,256]{2,1,0:T(8,128)(2,1)S(1)}, u32[]{:S(2)}, u32[]{:S(2)}) async-start(bf16[8,128,256]{2,1,0:T(8,128)(2,1)} %get-tuple-element.17), calls=%async_computation | async-start | bytes 1048576 | tf_op jit(solution)/shard_map/all_to_all | solution.py:34
  13.1 1.6 %collective-permute-start = (bf16[192,512]{1,0:T(8,128)(2,1)}, bf16[192,512]{1,0:T(8,128)(2,1)S(1)}, u32[]{:S(2)}, u32[]{:S(2)}) collective-permute-start(bf16[192,512]{1,0:T(8,128)(2,1)} %get-tuple-element.20), channel_id=1, source_target_pairs={{0,0},{1,1},{2,2},{3,3},{4,4},{5,5},{6,6},{7,7},{8,128},{9,129},{1... | collective-permute-start | bytes 589832 | tf_op jit(solution)/shard_map/ppermute | solution.py:57
  14.7 0.0 collective-permute-done.s0_ref
  14.7 15.1 %collective-permute-start.1 = (bf16[192,512]{1,0:T(8,128)(2,1)S(1)}, bf16[192,512]{1,0:T(8,128)(2,1)S(1)}, u32[]{:S(2)}, u32[]{:S(2)}) collective-permute-start(bf16[192,512]{1,0:T(8,128)(2,1)S(1)} %collective-permute-done.s0_ref), channel_id=1, source_target_pairs={{0,8},{1,9},{2,10},{3,11},{4,12},{5,13},{6,14},{7,15},{8,0},{9,1},... | collective-permute-start | bytes 589832 | tf_op jit(solution)/shard_map/ppermute | solution.py:57
  29.8 12.8 %collective-permute-start.2 = (bf16[192,512]{1,0:T(8,128)(2,1)S(1)}, bf16[192,512]{1,0:T(8,128)(2,1)S(1)}, u32[]{:S(2)}, u32[]{:S(2)}) collective-permute-start(bf16[192,512]{1,0:T(8,128)(2,1)S(1)} %collective-permute-done.s0_ref), channel_id=1, source_target_pairs={{0,16},{1,17},{2,18},{3,19},{4,20},{5,21},{6,22},{7,23},{8,24},{9,... | collective-permute-start | bytes 589832 | tf_op jit(solution)/shard_map/ppermute | solution.py:57
  42.6 2.2 %collective-permute-start.3 = (bf16[192,512]{1,0:T(8,128)(2,1)S(1)}, bf16[192,512]{1,0:T(8,128)(2,1)S(1)}, u32[]{:S(2)}, u32[]{:S(2)}) collective-permute-start(bf16[192,512]{1,0:T(8,128)(2,1)S(1)} %collective-permute-done.s0_ref), channel_id=1, source_target_pairs={{0,24},{1,25},{2,26},{3,27},{4,28},{5,29},{6,30},{7,31},{8,16},{9,... | collective-permute-start | bytes 589832 | tf_op jit(solution)/shard_map/ppermute | solution.py:57
  44.8 0.0 collective-permute-done.1.s1_ref
  44.8 4.2 %collective-permute-done.2.s2_ref = bf16[192,512]{1,0:T(8,128)(2,1)S(1)} collective-permute-done((bf16[192,512]{1,0:T(8,128)(2,1)S(1)}, bf16[192,512]{1,0:T(8,128)(2,1)S(1)}, u32[]{:S(2)}, u32[]{:S(2)}) %collective-permute-start.2) | collective-permute-done | bytes 196640 | tf_op jit(solution)/shard_map/ppermute | solution.py:57
  49.0 5.4 %collective-permute-done.3.s3_ref = bf16[192,512]{1,0:T(8,128)(2,1)S(1)} collective-permute-done((bf16[192,512]{1,0:T(8,128)(2,1)S(1)}, bf16[192,512]{1,0:T(8,128)(2,1)S(1)}, u32[]{:S(2)}, u32[]{:S(2)}) %collective-permute-start.3) | collective-permute-done | bytes 196640 | tf_op jit(solution)/shard_map/ppermute | solution.py:57
  54.4 0.1 pad_maximum_fusion
  54.5 2.4 %collective-permute-start.4 = (bf16[768,512]{1,0:T(8,128)(2,1)S(1)}, bf16[768,512]{1,0:T(8,128)(2,1)S(1)}, u32[]{:S(2)}, u32[]{:S(2)}) collective-permute-start(bf16[768,512]{1,0:T(8,128)(2,1)S(1)} %pad_maximum_fusion), channel_id=1, source_target_pairs={{0,64},{1,65},{2,66},{3,67},{4,68},{5,69},{6,70},{7,71},{8,72},{9,... | collective-permute-start | bytes 2359304 | tf_op jit(solution)/shard_map/ppermute | solution.py:57
  56.9 0.0 all-to-all-done
  56.9 0.1 convert_reduce_fusion
  57.0 22.5 %all_to_all.30 = f32[16,8,256]{2,1,0:T(8,128)S(1)} all-to-all(f32[16,8,256]{2,1,0:T(8,128)S(1)} %multiply_bitcast_fusion), channel_id=1, replica_groups=mesh['zl'=4,'co'=2,'zh'=2,'x'=4,'y'=8] {'zh','y'}, dimensions={0} | all-to-all | bytes 262144 | tf_op jit(solution)/shard_map/all_to_all | solution.py:34
  79.5 0.8 broadcast_in_dim.30
  80.3 3.5 %all-to-all-start.2 = ((f32[4,128,256]{2,1,0:T(8,128)}), f32[4,128,256]{2,1,0:T(8,128)S(1)}, u32[]{:S(2)}, u32[]{:S(2)}) async-start(f32[4,128,256]{2,1,0:T(8,128)} %broadcast_in_dim.30), calls=%async_computation.2 | async-start | bytes 1048576 | tf_op jit(solution)/shard_map/all_to_all | solution.py:34
  83.8 7.8 %all-to-all-done.2 = f32[4,128,256]{2,1,0:T(8,128)S(1)} async-done(((f32[4,128,256]{2,1,0:T(8,128)}), f32[4,128,256]{2,1,0:T(8,128)S(1)}, u32[]{:S(2)}, u32[]{:S(2)}) %all-to-all-start.2) | async-done | bytes 524320 | tf_op jit(solution)/shard_map/all_to_all | solution.py:34
  91.6 0.1 broadcast_in_dim.32
  91.7 6.8 %all_to_all.31.got_ref = f32[2,512,256]{2,1,0:T(8,128)S(1)} all-to-all(f32[2,512,256]{2,1,0:T(8,128)S(1)} %broadcast_in_dim.32), channel_id=1, replica_groups=mesh['zl'=4,'co'=2,'zh'=2,'x'=4,'y'=8] {'co'}, dimensions={0} | all-to-all | bytes 2097152 | tf_op jit(solution)/shard_map/all_to_all | solution.py:34
  98.5 0.8 shard_map.85
  99.3 0.7 collective-permute-start.5
  100.0 0.0 collective-permute-done.4.twin_ref
  100.0 10.1 %shard_map.86 = (bf16[64,40,128]{2,1,0:T(8,128)(2,1)}, bf16[64,512]{1,0:T(8,128)(2,1)S(1)}) custom-call(s32[1]{0:T(128)} %bitcast.own_ref, f32[512,512]{1,0:T(8,128)S(1)} %get-tuple-element.18.g_ref, f32[2,512,512]{2,1,0:T(8,128)S(1)} %get-tuple-element.19.gram_ref, bf16[192,512]{1,0:T(8,128)(2,1)S(1)} %collective-permute-done.s0_ref, ...), custom_call_target="tpu_custom_call" | custom-call | flops 6979321856 | bytes 1048576 | tf_op jit(solution)/shard_map/pallas_call | solution.py:340
  110.0 0.0 collective-permute-done.5
  110.0 9.6 %all-to-all-start.4 = ((bf16[64,40,128]{2,1,0:T(8,128)(2,1)}), bf16[64,40,128]{2,1,0:T(8,128)(2,1)S(1)}, u32[]{:S(2)}, u32[]{:S(2)}) async-start(bf16[64,40,128]{2,1,0:T(8,128)(2,1)} %get-tuple-element.24), calls=%async_computation.4 | async-start | bytes 1310720 | tf_op jit(solution)/shard_map/all_to_all | solution.py:34
  119.6 0.0 copy-start
  119.6 0.0 copy-start.1
  119.6 0.8 collective-permute-start.6
  120.4 17.5 %all-to-all-done.4.got_ref = bf16[64,40,128]{2,1,0:T(8,128)(2,1)S(1)} async-done(((bf16[64,40,128]{2,1,0:T(8,128)(2,1)}), bf16[64,40,128]{2,1,0:T(8,128)(2,1)S(1)}, u32[]{:S(2)}, u32[]{:S(2)}) %all-to-all-start.4) | async-done | bytes 655392 | tf_op jit(solution)/shard_map/all_to_all | solution.py:34
  138.0 0.4 shard_map.87
  138.4 0.9 broadcast_in_dim.33
  139.2 0.0 copy-start.2
  139.2 6.7 %all-to-all-start.5 = ((bf16[2,8,8,2048]{3,2,1,0:T(8,128)(2,1)}), bf16[2,8,8,2048]{3,2,1,0:T(8,128)(2,1)S(1)}, u32[]{:S(2)}, u32[]{:S(2)}) async-start(bf16[2,8,8,2048]{3,2,1,0:T(8,128)(2,1)} %broadcast_in_dim.33), calls=%async_computation.5 | async-start | bytes 1048576 | tf_op jit(solution)/shard_map/all_to_all | solution.py:34
  145.9 0.0 copy-done
  145.9 0.0 copy-done.1
  145.9 0.7 add_bitcast_fusion
  146.7 0.5 slice.9
  147.2 0.1 all-to-all-done.5.got_ref
  147.3 0.8 shard_map.88
  148.1 0.0 collective-permute-done.6
  148.1 0.0 copy-done.2
  148.1 1.2 add_bitcast_fusion.2
  (1 shorter events, 0.0 us)
Async XLA Ops:
  2.9 54.0 %all-to-all-start = ((bf16[8,128,256]{2,1,0:T(8,128)(2,1)}), bf16[8,128,256]{2,1,0:T(8,128)(2,1)S(1)}, u32[]{:S(2)}, u32[]{:S(2)}) async-start(bf16[8,128,256]{2,1,0:T(8,128)(2,1)} %get-tuple-element.17), calls=%async_computation | async-start | bytes 1048576 | tf_op jit(solution)/shard_map/all_to_all | solution.py:34
  13.1 1.6 %collective-permute-start = (bf16[192,512]{1,0:T(8,128)(2,1)}, bf16[192,512]{1,0:T(8,128)(2,1)S(1)}, u32[]{:S(2)}, u32[]{:S(2)}) collective-permute-start(bf16[192,512]{1,0:T(8,128)(2,1)} %get-tuple-element.20), channel_id=1, source_target_pairs={{0,0},{1,1},{2,2},{3,3},{4,4},{5,5},{6,6},{7,7},{8,128},{9,129},{1... | collective-permute-start | bytes 589832 | tf_op jit(solution)/shard_map/ppermute | solution.py:57
  14.7 30.1 %collective-permute-start.1 = (bf16[192,512]{1,0:T(8,128)(2,1)S(1)}, bf16[192,512]{1,0:T(8,128)(2,1)S(1)}, u32[]{:S(2)}, u32[]{:S(2)}) collective-permute-start(bf16[192,512]{1,0:T(8,128)(2,1)S(1)} %collective-permute-done.s0_ref), channel_id=1, source_target_pairs={{0,8},{1,9},{2,10},{3,11},{4,12},{5,13},{6,14},{7,15},{8,0},{9,1},... | collective-permute-start | bytes 589832 | tf_op jit(solution)/shard_map/ppermute | solution.py:57
  29.8 19.2 %collective-permute-start.2 = (bf16[192,512]{1,0:T(8,128)(2,1)S(1)}, bf16[192,512]{1,0:T(8,128)(2,1)S(1)}, u32[]{:S(2)}, u32[]{:S(2)}) collective-permute-start(bf16[192,512]{1,0:T(8,128)(2,1)S(1)} %collective-permute-done.s0_ref), channel_id=1, source_target_pairs={{0,16},{1,17},{2,18},{3,19},{4,20},{5,21},{6,22},{7,23},{8,24},{9,... | collective-permute-start | bytes 589832 | tf_op jit(solution)/shard_map/ppermute | solution.py:57
  42.6 11.8 %collective-permute-start.3 = (bf16[192,512]{1,0:T(8,128)(2,1)S(1)}, bf16[192,512]{1,0:T(8,128)(2,1)S(1)}, u32[]{:S(2)}, u32[]{:S(2)}) collective-permute-start(bf16[192,512]{1,0:T(8,128)(2,1)S(1)} %collective-permute-done.s0_ref), channel_id=1, source_target_pairs={{0,24},{1,25},{2,26},{3,27},{4,28},{5,29},{6,30},{7,31},{8,16},{9,... | collective-permute-start | bytes 589832 | tf_op jit(solution)/shard_map/ppermute | solution.py:57
  54.5 45.5 %collective-permute-start.4 = (bf16[768,512]{1,0:T(8,128)(2,1)S(1)}, bf16[768,512]{1,0:T(8,128)(2,1)S(1)}, u32[]{:S(2)}, u32[]{:S(2)}) collective-permute-start(bf16[768,512]{1,0:T(8,128)(2,1)S(1)} %pad_maximum_fusion), channel_id=1, source_target_pairs={{0,64},{1,65},{2,66},{3,67},{4,68},{5,69},{6,70},{7,71},{8,72},{9,... | collective-permute-start | bytes 2359304 | tf_op jit(solution)/shard_map/ppermute | solution.py:57
  80.3 11.3 %all-to-all-start.2 = ((f32[4,128,256]{2,1,0:T(8,128)}), f32[4,128,256]{2,1,0:T(8,128)S(1)}, u32[]{:S(2)}, u32[]{:S(2)}) async-start(f32[4,128,256]{2,1,0:T(8,128)} %broadcast_in_dim.30), calls=%async_computation.2 | async-start | bytes 1048576 | tf_op jit(solution)/shard_map/all_to_all | solution.py:34
  99.3 10.7 %collective-permute-start.5 = (bf16[128,512]{1,0:T(8,128)(2,1)S(1)}, bf16[128,512]{1,0:T(8,128)(2,1)S(1)}, u32[]{:S(2)}, u32[]{:S(2)}) collective-permute-start(bf16[128,512]{1,0:T(8,128)(2,1)S(1)} %get-tuple-element.22), channel_id=1, source_target_pairs={{0,0},{1,1},{2,2},{3,3},{4,4},{5,5},{6,6},{7,7},{8,128},{9,129},{1... | collective-permute-start | bytes 393224 | tf_op jit(solution)/shard_map/ppermute | solution.py:57
  110.0 27.9 %all-to-all-start.4 = ((bf16[64,40,128]{2,1,0:T(8,128)(2,1)}), bf16[64,40,128]{2,1,0:T(8,128)(2,1)S(1)}, u32[]{:S(2)}, u32[]{:S(2)}) async-start(bf16[64,40,128]{2,1,0:T(8,128)(2,1)} %get-tuple-element.24), calls=%async_computation.4 | async-start | bytes 1310720 | tf_op jit(solution)/shard_map/all_to_all | solution.py:34
  119.6 26.3 %copy-start = (f32[1,64,512]{2,1,0:T(8,128)S(1)}, f32[1,64,512]{2,1,0:T(8,128)}, u32[]{:S(2)}) copy-start(f32[1,64,512]{2,1,0:T(8,128)} %param.6) | copy-start | bytes 393220
  119.6 26.3 %copy-start.1 = (f32[1,64,512]{2,1,0:T(8,128)S(1)}, f32[1,64,512]{2,1,0:T(8,128)}, u32[]{:S(2)}) copy-start(f32[1,64,512]{2,1,0:T(8,128)} %param.7) | copy-start | bytes 393220
  119.6 28.5 %collective-permute-start.6 = (bf16[64,512]{1,0:T(8,128)(2,1)S(1)}, bf16[64,512]{1,0:T(8,128)(2,1)S(1)}, u32[]{:S(2)}, u32[]{:S(2)}) collective-permute-start(bf16[64,512]{1,0:T(8,128)(2,1)S(1)} %get-tuple-element.28), channel_id=1, source_target_pairs={{0,0},{1,1},{2,2},{3,3},{4,4},{5,5},{6,6},{7,7},{8,128},{9,129},{1... | collective-permute-start | bytes 196616 | tf_op jit(solution)/shard_map/ppermute | solution.py:57
  139.2 8.9 %copy-start.2 = (f32[1,64,512]{2,1,0:T(8,128)S(1)}, f32[1,64,512]{2,1,0:T(8,128)}, u32[]{:S(2)}) copy-start(f32[1,64,512]{2,1,0:T(8,128)} %param.8) | copy-start | bytes 393220
  139.2 8.1 %all-to-all-start.5 = ((bf16[2,8,8,2048]{3,2,1,0:T(8,128)(2,1)}), bf16[2,8,8,2048]{3,2,1,0:T(8,128)(2,1)S(1)}, u32[]{:S(2)}, u32[]{:S(2)}) async-start(bf16[2,8,8,2048]{3,2,1,0:T(8,128)(2,1)} %broadcast_in_dim.33), calls=%async_computation.5 | async-start | bytes 1048576 | tf_op jit(solution)/shard_map/all_to_all | solution.py:34

commit v5 on v3

--- a/solution.py
+++ b/solution.py
@@ -99,23 +99,8 @@
                 out_ref[i % 4 * 2 + w // 2, at : at + N, lanes] = rows.astype(BF16)
 
 
-def gram_kernel(own_ref, got_ref, g_ref, gram_ref, ret_ref, g_b):
-    own = pl.multiple_of(own_ref[0] * ROWS, ROWS)
-    for half in range(2):
-        for x in range(4):
-            for zh in range(2):
-                rows = slice((zh * 4 + x) * ROWS, (zh * 4 + x + 1) * ROWS)
-                part = got_ref[half, (x * 2 + zh) * ROWS : (x * 2 + zh + 1) * ROWS, :]
-                cols = slice(half * HALF, (half + 1) * HALF)
-                g_ref[rows, cols] = part
-                g_b[rows, cols] = part.astype(BF16)
-    for side in range(2):
-        gram_ref[side] = dot(g_b[...], g_b[...], (((1,), (1,)), ((0,), (0,)))[side])
-        ret_ref[side * ROWS : (side + 1) * ROWS, :] = gram_ref[side, pl.ds(own, ROWS), :].astype(BF16)
-
-
 def block_kernel(
-    own_ref, g_ref, gram_ref, s0_ref, s1_ref, s2_ref, s3_ref, twin_ref,
+    own_ref, got_ref, s0_ref, s1_ref, s2_ref, s3_ref, twin_ref,
     msg_ref, ret_ref, m_f, m_b, v_b, w_f, w_b, y_f, y_b, z_b, base_f,
 ):
     own = pl.multiple_of(own_ref[0] * ROWS, ROWS)
@@ -124,22 +109,30 @@
     chunk = BLOCK // 2
     spans = [pl.ds(k * chunk, chunk) for k in range(2)]
     norm_g = jnp.zeros((1, 1), F32)
-    for rows in spans:
-        part = g_ref[rows, :]
-        norm_g += jnp.sum(part * part, keepdims=True)
-        y_f[rows, :] = part
-        y_b[rows, :] = part.astype(BF16)
+    for half in range(2):
+        cols = slice(half * HALF, (half + 1) * HALF)
+        for k in range(4):
+            for zh in range(2):
+                at = (k * 2 + zh) * ROWS
+                part = got_ref[half, at : at + ROWS, :]
+                norm_g += jnp.sum(part * part, keepdims=True)
+                rows = slice((zh * 4 + k) * ROWS, (zh * 4 + k + 1) * ROWS)
+                y_f[rows, cols] = part
+                y_b[rows, cols] = part.astype(BF16)
     shares = []
     for flip, ref in enumerate((s0_ref, s1_ref, s2_ref, s3_ref)):
         shares.append((pl.multiple_of((own_ref[0] ^ (2 * flip)) * ROWS, ROWS), ref, 0))
         shares.append((pl.multiple_of((own_ref[0] ^ (2 * flip + 1)) * ROWS, ROWS), twin_ref, flip * SHARE))
     scale = jnp.ones((1, 1), F32)
     for side in range(2):
+        w_f[side] = dot(y_b[...], y_b[...], (((1,), (1,)), ((0,), (0,)))[side])
+        rows = w_f[side, pl.ds(own, ROWS), :]
+        ret_ref[(1 + side) * ROWS : (2 + side) * ROWS, :] = rows.astype(BF16)
         total = jnp.zeros((1, 1), F32)
         for at, ref, start in shares:
             rows = pl.ds(at, ROWS)
             old = ref[start + side * ROWS : start + (side + 1) * ROWS, :].astype(F32)
-            new = stat_decay * old + (1.0 - stat_decay) * gram_ref[side, rows, :]
+            new = stat_decay * old + (1.0 - stat_decay) * w_f[side, rows, :]
             m_f[side, rows, :] = new
             total += jnp.sum(new * new, keepdims=True)
         frob = jnp.sqrt(total)
@@ -187,7 +180,7 @@
         new = y_f[rows, :] * scale
         norm_p += jnp.sum(new * new, keepdims=True)
         y_f[rows, :] = new
-    ret_ref[...] = y_f[pl.ds(own, ROWS), :].astype(BF16)
+    ret_ref[0:ROWS, :] = y_f[pl.ds(own, ROWS), :].astype(BF16)
     lane = lax.broadcasted_iota(jnp.int32, (N, LANES), 1)
     norms = jnp.zeros((N, LANES), F32)
     for k, part in enumerate(three_parts(norm_p) + three_parts(norm_g)):
@@ -208,7 +201,7 @@
                 msg_ref[(z * 2 + zh) * N + row, 4 * N : 5 * N, :] = norms
 
 
-def weight_kernel(got_ref, ret_ref, mom_ref, half_ref, mom_out_ref, rows_f):
+def weight_kernel(got_ref, half_ref, graft_ref, rows_f):
     total = jnp.zeros((N, LANES), F32)
     for k in range(8 * N):
         total += got_ref[k, 4 * N : 5 * N, :].astype(F32)
@@ -231,7 +224,7 @@
             for w in range(2):
                 cols = slice(j * HALF + w * LANES, j * HALF + (w + 1) * LANES)
                 half_ref[p, :, cols] = rows_f[slot, w, pl.ds(p, N, stride=N), :].astype(BF16)
-    mom_out_ref[...] = moment_decay * mom_ref[...] + graft * ret_ref[...].astype(F32)
+    graft_ref[...] = jnp.broadcast_to(graft, (N, LANES))
 
 
 def join_kernel(got_ref, out_ref):
@@ -269,7 +262,6 @@
     s0 = turned(share)
     shares = [s0] + [along_x(s0, flip) for flip in (1, 2, 3)]
     twin = other_core(jnp.concatenate(shares, axis=0))
-
     (pieces,) = call(
         pack_kernel, [((N, 2 * ROWS, HALF), BF16)], [scratch(4, ROWS, LANES, dtype=F32)], mib=8
     )(gradients[0])
@@ -278,19 +270,9 @@
     mean = exchanged(mean.reshape(2 * N, N, HALF), PLANE)
     mean = spread(mean.reshape(2 * ROWS, HALF), "x")
     mean = spread(mean.reshape(BLOCK, HALF), "co")
-
-    mean, grams, ret = call(
-        gram_kernel,
-        [((BLOCK, BLOCK), F32), ((2, BLOCK, BLOCK), F32), ((2 * ROWS, BLOCK), BF16)],
-        [scratch(BLOCK, BLOCK, dtype=BF16)],
-        flops=4 * BLOCK**3,
-        scalars=1,
-        mib=16,
-    )(own, mean)
-    ret = turned(ret)
     update = call(
         block_kernel,
-        [((8 * N, MESSAGE, LANES), BF16), ((ROWS, BLOCK), BF16)],
+        [((8 * N, MESSAGE, LANES), BF16), ((SHARE, BLOCK), BF16)],
         [
             scratch(2, BLOCK, BLOCK, dtype=F32),
             scratch(2, BLOCK, BLOCK, dtype=BF16),
@@ -302,24 +284,25 @@
             scratch(BLOCK, BLOCK, dtype=BF16),
             scratch(BLOCK, BLOCK, dtype=F32),
         ],
-        flops=52 * BLOCK**3,
+        flops=56 * BLOCK**3,
         scalars=1,
-        arrays=7,
+        arrays=6,
     )
-    messages, rows = update(own, mean, grams, *shares, twin)
-    rows = turned(rows)
+    messages, ret = update(own, mean, *shares, twin)
+    ret = turned(ret)
     got = exchanged(messages, SOLID)
-    half, moment_rows = call(
+    half, graft = call(
         weight_kernel,
-        [((N, N, N * HALF), BF16), ((ROWS, BLOCK), F32)],
+        [((N, N, N * HALF), BF16), ((N, LANES), F32)],
         [scratch(2, 2, ROWS, LANES, dtype=F32)],
-        arrays=3,
         mib=16,
-    )(got, rows, momentum[0])
+    )(got)
     half = spread(half, "co")
     (params,) = call(join_kernel, [((N, N, N * BLOCK), BF16)], [], mib=8)(half)
-    left_next = stat_decay * left_stat[0] + (1.0 - stat_decay) * ret[:ROWS].astype(F32)
-    right_next = stat_decay * right_stat[0] + (1.0 - stat_decay) * ret[ROWS:].astype(F32)
+    ret, graft = lax.optimization_barrier((ret, graft))
+    moment_rows = moment_decay * momentum[0] + graft[0, 0] * ret[:ROWS].astype(F32)
+    left_next = stat_decay * left_stat[0] + (1.0 - stat_decay) * ret[ROWS : 2 * ROWS].astype(F32)
+    right_next = stat_decay * right_stat[0] + (1.0 - stat_decay) * ret[2 * ROWS :].astype(F32)
     return (params, moment_rows[None], left_next[None], right_next[None])
 
 

time: 153 us -> 156 us (1.020)
  blocking collectives: 33.4 us -> 22.6 us
  starting transfers between devices: 49.6 us -> 60.4 us
  local copies, waits for them, and re-layouts: 2 us -> 4.34 us
  other arithmetic: 0.93 us -> 2.49 us
    ppermute x7 -> x6, waiting for transfers between devices: 44.4 us -> 26.5 us  [moved(): return lax.ppermute(shard, ALL, pairs)]
    all_to_all x3 -> x5, waiting for transfers between devices: 6.89 us -> 24.7 us  [exchanged(): return lax.all_to_all(pieces, axis, split_axis=0, concat_axis=0, tiled=True)]
    all_to_all x3 -> x1, blocking collectives: 33.4 us -> 22.6 us  [exchanged(): return lax.all_to_all(pieces, axis, split_axis=0, concat_axis=0, tiled=True)]
    all_to_all x3 -> x5, starting transfers between devices: 20.9 us -> 31.3 us  [exchanged(): return lax.all_to_all(pieces, axis, split_axis=0, concat_axis=0, tiled=True)]
    broadcast_in_dim x3, local copies, waits for them, and re-layouts: 0.95 us -> 2.75 us  [spread(): copies = jnp.broadcast_to(shard[None], (lax.axis_size(axis), *shard.shape))]
    pallas_call x3 -> x2, Pallas kernels: 11.9 us -> 11.1 us  [the longest x1 10.7 us: step(): messages, ret = update(own, mean, *shares, twin)]
    ppermute x7 -> x6, starting transfers between devices: 28.7 us -> 29.1 us  [moved(): return lax.ppermute(shard, ALL, pairs)]
  transfers between devices with their start and end apart: 10 -> 11, of which waited for: 6 -> 7; matrix products, arithmetic and copies ran while one was open for 1% -> 3% of each run, Pallas kernels for 1% -> 0%
where the time goes in v5:
time: 156 us; the launch traced here: 155 us
  starting transfers between devices  60.4 us (39%)
  waiting for transfers between devices  51.3 us (33%)
  blocking collectives  22.6 us (14%)
  Pallas kernels  12.9 us (8%)
  local copies, waits for them, and re-layouts  4.34 us (3%)
  other arithmetic  2.49 us (2%)
    all_to_all x5, starting transfers between devices, exchanged(): return lax.all_to_all(pieces, axis, split_axis=0, concat_axis=0, tiled=True)  31.3 us
    ppermute x6, starting transfers between devices, moved(): return lax.ppermute(shard, ALL, pairs)  29.1 us
    ppermute x6, waiting for transfers between devices, moved(): return lax.ppermute(shard, ALL, pairs)  26.5 us
    all_to_all x5, waiting for transfers between devices, exchanged(): return lax.all_to_all(pieces, axis, split_axis=0, concat_axis=0, tiled=True)  24.7 us
    all_to_all x1, blocking collectives, exchanged(): return lax.all_to_all(pieces, axis, split_axis=0, concat_axis=0, tiled=True)  22.6 us
    pallas_call x1, Pallas kernels, step(): messages, ret = update(own, mean, *shares, twin)  10.7 us
  transfers between devices with their start and end apart: 11, of which 7 were waited for; matrix products, arithmetic and copies ran while one was open for 3% of the time, Pallas kernels for 0%

profile of v5, /device:TPU:27, one launch (start us, length us, event | category | flops | bytes accessed | tf_op | source)
XLA Modules:
  0.0 154.8 jit_solution(10471915051498777356)
XLA Ops:
  0.6 0.0 copy-start
  0.6 1.0 copy-done
  1.7 0.0 copy-start.1
  1.7 0.0 copy-start.2
  1.7 0.0 copy-start.3
  1.7 0.0 copy-start.4
  1.7 1.1 shard_map.84
  2.7 7.9 %all-to-all-start = ((bf16[8,128,256]{2,1,0:T(8,128)(2,1)}), bf16[8,128,256]{2,1,0:T(8,128)(2,1)S(1)}, u32[]{:S(2)}, u32[]{:S(2)}) async-start(bf16[8,128,256]{2,1,0:T(8,128)(2,1)} %shard_map.84), calls=%async_computation | async-start | bytes 1048576 | tf_op jit(solution)/shard_map/all_to_all | solution.py:34
  10.7 0.0 copy-done.1
  10.7 0.0 copy-done.2
  10.7 0.0 copy-done.3
  10.7 0.0 copy-done.4
  10.8 3.2 %collective-permute-start = (bf16[192,512]{1,0:T(8,128)(2,1)S(1)}, bf16[192,512]{1,0:T(8,128)(2,1)S(1)}, u32[]{:S(2)}, u32[]{:S(2)}) collective-permute-start(bf16[192,512]{1,0:T(8,128)(2,1)S(1)} %pad_maximum_fusion.1), channel_id=1, source_target_pairs={{0,0},{1,1},{2,2},{3,3},{4,4},{5,5},{6,6},{7,7},{8,128},{9,129},{1... | collective-permute-start | bytes 589832 | tf_op jit(solution)/shard_map/ppermute | solution.py:57
  14.0 11.0 %collective-permute-done.s0_ref = bf16[192,512]{1,0:T(8,128)(2,1)S(1)} collective-permute-done((bf16[192,512]{1,0:T(8,128)(2,1)S(1)}, bf16[192,512]{1,0:T(8,128)(2,1)S(1)}, u32[]{:S(2)}, u32[]{:S(2)}) %collective-permute-start) | collective-permute-done | bytes 196640 | tf_op jit(solution)/shard_map/ppermute | solution.py:57
  25.0 11.6 %collective-permute-start.3 = (bf16[192,512]{1,0:T(8,128)(2,1)S(1)}, bf16[192,512]{1,0:T(8,128)(2,1)S(1)}, u32[]{:S(2)}, u32[]{:S(2)}) collective-permute-start(bf16[192,512]{1,0:T(8,128)(2,1)S(1)} %collective-permute-done.s0_ref), channel_id=1, source_target_pairs={{0,24},{1,25},{2,26},{3,27},{4,28},{5,29},{6,30},{7,31},{8,16},{9,... | collective-permute-start | bytes 589832 | tf_op jit(solution)/shard_map/ppermute | solution.py:57
  36.6 1.9 %collective-permute-start.2 = (bf16[192,512]{1,0:T(8,128)(2,1)S(1)}, bf16[192,512]{1,0:T(8,128)(2,1)S(1)}, u32[]{:S(2)}, u32[]{:S(2)}) collective-permute-start(bf16[192,512]{1,0:T(8,128)(2,1)S(1)} %collective-permute-done.s0_ref), channel_id=1, source_target_pairs={{0,16},{1,17},{2,18},{3,19},{4,20},{5,21},{6,22},{7,23},{8,24},{9,... | collective-permute-start | bytes 589832 | tf_op jit(solution)/shard_map/ppermute | solution.py:57
  38.5 3.7 %collective-permute-start.1 = (bf16[192,512]{1,0:T(8,128)(2,1)S(1)}, bf16[192,512]{1,0:T(8,128)(2,1)S(1)}, u32[]{:S(2)}, u32[]{:S(2)}) collective-permute-start(bf16[192,512]{1,0:T(8,128)(2,1)S(1)} %collective-permute-done.s0_ref), channel_id=1, source_target_pairs={{0,8},{1,9},{2,10},{3,11},{4,12},{5,13},{6,14},{7,15},{8,0},{9,1},... | collective-permute-start | bytes 589832 | tf_op jit(solution)/shard_map/ppermute | solution.py:57
  42.2 0.0 collective-permute-done.3.s3_ref
  42.3 2.9 %collective-permute-done.2.s2_ref = bf16[192,512]{1,0:T(8,128)(2,1)S(1)} collective-permute-done((bf16[192,512]{1,0:T(8,128)(2,1)S(1)}, bf16[192,512]{1,0:T(8,128)(2,1)S(1)}, u32[]{:S(2)}, u32[]{:S(2)}) %collective-permute-start.2) | collective-permute-done | bytes 196640 | tf_op jit(solution)/shard_map/ppermute | solution.py:57
  45.2 2.5 %collective-permute-done.1.s1_ref = bf16[192,512]{1,0:T(8,128)(2,1)S(1)} collective-permute-done((bf16[192,512]{1,0:T(8,128)(2,1)S(1)}, bf16[192,512]{1,0:T(8,128)(2,1)S(1)}, u32[]{:S(2)}, u32[]{:S(2)}) %collective-permute-start.1) | collective-permute-done | bytes 196640 | tf_op jit(solution)/shard_map/ppermute | solution.py:57
  47.7 1.0 pad_maximum_fusion
  48.6 4.7 %collective-permute-start.4 = (bf16[768,512]{1,0:T(8,128)(2,1)}, bf16[768,512]{1,0:T(8,128)(2,1)S(1)}, u32[]{:S(2)}, u32[]{:S(2)}) collective-permute-start(bf16[768,512]{1,0:T(8,128)(2,1)} %pad_maximum_fusion), channel_id=1, source_target_pairs={{0,64},{1,65},{2,66},{3,67},{4,68},{5,69},{6,70},{7,71},{8,72},{9,... | collective-permute-start | bytes 2359304 | tf_op jit(solution)/shard_map/ppermute | solution.py:57
  53.3 0.0 all-to-all-done
  53.3 0.1 convert_reduce_fusion
  53.4 22.6 %all_to_all.30 = f32[16,8,256]{2,1,0:T(8,128)S(1)} all-to-all(f32[16,8,256]{2,1,0:T(8,128)S(1)} %multiply_bitcast_fusion), channel_id=1, replica_groups=mesh['zl'=4,'co'=2,'zh'=2,'x'=4,'y'=8] {'zh','y'}, dimensions={0} | all-to-all | bytes 262144 | tf_op jit(solution)/shard_map/all_to_all | solution.py:34
  76.0 0.8 broadcast_in_dim.30
  76.8 4.5 %all-to-all-start.2 = ((f32[4,128,256]{2,1,0:T(8,128)}), f32[4,128,256]{2,1,0:T(8,128)S(1)}, u32[]{:S(2)}, u32[]{:S(2)}) async-start(f32[4,128,256]{2,1,0:T(8,128)} %broadcast_in_dim.30), calls=%async_computation.2 | async-start | bytes 1048576 | tf_op jit(solution)/shard_map/all_to_all | solution.py:34
  81.3 6.6 %all-to-all-done.2 = f32[4,128,256]{2,1,0:T(8,128)S(1)} async-done(((f32[4,128,256]{2,1,0:T(8,128)}), f32[4,128,256]{2,1,0:T(8,128)S(1)}, u32[]{:S(2)}, u32[]{:S(2)}) %all-to-all-start.2) | async-done | bytes 524320 | tf_op jit(solution)/shard_map/all_to_all | solution.py:34
  87.9 1.1 broadcast_in_dim.32
  89.0 6.2 %all-to-all-start.3 = ((f32[2,512,256]{2,1,0:T(8,128)}), f32[2,512,256]{2,1,0:T(8,128)S(1)}, u32[]{:S(2)}, u32[]{:S(2)}) async-start(f32[2,512,256]{2,1,0:T(8,128)} %broadcast_in_dim.32), calls=%async_computation.3 | async-start | bytes 2097152 | tf_op jit(solution)/shard_map/all_to_all | solution.py:34
  95.2 0.0 collective-permute-done.4.twin_ref
  95.2 1.7 %all-to-all-done.3.got_ref = f32[2,512,256]{2,1,0:T(8,128)S(1)} async-done(((f32[2,512,256]{2,1,0:T(8,128)}), f32[2,512,256]{2,1,0:T(8,128)S(1)}, u32[]{:S(2)}, u32[]{:S(2)}) %all-to-all-start.3) | async-done | bytes 1048608 | tf_op jit(solution)/shard_map/all_to_all | solution.py:34
  96.9 10.7 %shard_map.85 = (bf16[64,40,128]{2,1,0:T(8,128)(2,1)}, bf16[192,512]{1,0:T(8,128)(2,1)S(1)}) custom-call(s32[1]{0:T(128)} %bitcast.own_ref, f32[2,512,256]{2,1,0:T(8,128)S(1)} %all-to-all-done.3.got_ref, bf16[192,512]{1,0:T(8,128)(2,1)S(1)} %collective-permute-done.s0_ref, bf16[192,512]{1,0:T(8,128)(2,1)S(1)} %collective-permute-done.1.s1_ref, ...), custom_call_target="tpu_custom_call" | custom-call | flops 7516192768 | bytes 1048576 | tf_op jit(solution)/shard_map/pallas_call | solution.py:291
  107.6 8.8 %all-to-all-start.4 = ((bf16[64,40,128]{2,1,0:T(8,128)(2,1)}), bf16[64,40,128]{2,1,0:T(8,128)(2,1)S(1)}, u32[]{:S(2)}, u32[]{:S(2)}) async-start(bf16[64,40,128]{2,1,0:T(8,128)(2,1)} %get-tuple-element.10), calls=%async_computation.4 | async-start | bytes 1310720 | tf_op jit(solution)/shard_map/all_to_all | solution.py:34
  116.4 4.0 %collective-permute-start.5 = (bf16[192,512]{1,0:T(8,128)(2,1)S(1)}, bf16[192,512]{1,0:T(8,128)(2,1)S(1)}, u32[]{:S(2)}, u32[]{:S(2)}) collective-permute-start(bf16[192,512]{1,0:T(8,128)(2,1)S(1)} %get-tuple-element.12), channel_id=1, source_target_pairs={{0,0},{1,1},{2,2},{3,3},{4,4},{5,5},{6,6},{7,7},{8,128},{9,129},{1... | collective-permute-start | bytes 589832 | tf_op jit(solution)/shard_map/ppermute | solution.py:57
  120.4 16.4 %all-to-all-done.4.got_ref = bf16[64,40,128]{2,1,0:T(8,128)(2,1)S(1)} async-done(((bf16[64,40,128]{2,1,0:T(8,128)(2,1)}), bf16[64,40,128]{2,1,0:T(8,128)(2,1)S(1)}, u32[]{:S(2)}, u32[]{:S(2)}) %all-to-all-start.4) | async-done | bytes 655392 | tf_op jit(solution)/shard_map/all_to_all | solution.py:34
  136.8 0.4 shard_map.86
  137.2 10.1 %collective-permute-done.5 = bf16[192,512]{1,0:T(8,128)(2,1)S(1)} collective-permute-done((bf16[192,512]{1,0:T(8,128)(2,1)S(1)}, bf16[192,512]{1,0:T(8,128)(2,1)S(1)}, u32[]{:S(2)}, u32[]{:S(2)}) %collective-permute-start.5) | collective-permute-done | bytes 196640 | tf_op jit(solution)/shard_map/ppermute | solution.py:57
  147.3 0.5 slice.12
  147.8 0.8 broadcast_in_dim.33
  148.7 4.0 %all-to-all-start.5 = ((bf16[2,8,8,2048]{3,2,1,0:T(8,128)(2,1)}), bf16[2,8,8,2048]{3,2,1,0:T(8,128)(2,1)S(1)}, u32[]{:S(2)}, u32[]{:S(2)}) async-start(bf16[2,8,8,2048]{3,2,1,0:T(8,128)(2,1)} %broadcast_in_dim.33), calls=%async_computation.5 | async-start | bytes 1048576 | tf_op jit(solution)/shard_map/all_to_all | solution.py:34
  152.6 1.4 fusion
  154.0 0.0 all-to-all-done.5.got_ref
  154.0 0.8 shard_map.87
  (4 shorter events, 0.1 us)
Async XLA Ops:
  0.6 1.0 copy-start
  1.7 9.0 %copy-start.1 = (f32[1,64,512]{2,1,0:T(8,128)S(1)}, f32[1,64,512]{2,1,0:T(8,128)}, u32[]{:S(2)}) copy-start(f32[1,64,512]{2,1,0:T(8,128)} %param.6) | copy-start | bytes 393220
  1.7 9.0 %copy-start.2 = (f32[1,64,512]{2,1,0:T(8,128)S(1)}, f32[1,64,512]{2,1,0:T(8,128)}, u32[]{:S(2)}) copy-start(f32[1,64,512]{2,1,0:T(8,128)} %param.8) | copy-start | bytes 393220
  1.7 9.0 %copy-start.3 = (f32[1,64,512]{2,1,0:T(8,128)S(1)}, f32[1,64,512]{2,1,0:T(8,128)}, u32[]{:S(2)}) copy-start(f32[1,64,512]{2,1,0:T(8,128)} %param.7) | copy-start | bytes 393220
  1.7 9.0 %copy-start.4 = (f32[1,64,512]{2,1,0:T(8,128)S(1)}, f32[1,64,512]{2,1,0:T(8,128)}, u32[]{:S(2)}) copy-start(f32[1,64,512]{2,1,0:T(8,128)} %param.9) | copy-start | bytes 393220
  2.7 50.5 %all-to-all-start = ((bf16[8,128,256]{2,1,0:T(8,128)(2,1)}), bf16[8,128,256]{2,1,0:T(8,128)(2,1)S(1)}, u32[]{:S(2)}, u32[]{:S(2)}) async-start(bf16[8,128,256]{2,1,0:T(8,128)(2,1)} %shard_map.84), calls=%async_computation | async-start | bytes 1048576 | tf_op jit(solution)/shard_map/all_to_all | solution.py:34
  10.8 14.2 %collective-permute-start = (bf16[192,512]{1,0:T(8,128)(2,1)S(1)}, bf16[192,512]{1,0:T(8,128)(2,1)S(1)}, u32[]{:S(2)}, u32[]{:S(2)}) collective-permute-start(bf16[192,512]{1,0:T(8,128)(2,1)S(1)} %pad_maximum_fusion.1), channel_id=1, source_target_pairs={{0,0},{1,1},{2,2},{3,3},{4,4},{5,5},{6,6},{7,7},{8,128},{9,129},{1... | collective-permute-start | bytes 589832 | tf_op jit(solution)/shard_map/ppermute | solution.py:57
  25.0 17.2 %collective-permute-start.3 = (bf16[192,512]{1,0:T(8,128)(2,1)S(1)}, bf16[192,512]{1,0:T(8,128)(2,1)S(1)}, u32[]{:S(2)}, u32[]{:S(2)}) collective-permute-start(bf16[192,512]{1,0:T(8,128)(2,1)S(1)} %collective-permute-done.s0_ref), channel_id=1, source_target_pairs={{0,24},{1,25},{2,26},{3,27},{4,28},{5,29},{6,30},{7,31},{8,16},{9,... | collective-permute-start | bytes 589832 | tf_op jit(solution)/shard_map/ppermute | solution.py:57
  36.6 8.6 %collective-permute-start.2 = (bf16[192,512]{1,0:T(8,128)(2,1)S(1)}, bf16[192,512]{1,0:T(8,128)(2,1)S(1)}, u32[]{:S(2)}, u32[]{:S(2)}) collective-permute-start(bf16[192,512]{1,0:T(8,128)(2,1)S(1)} %collective-permute-done.s0_ref), channel_id=1, source_target_pairs={{0,16},{1,17},{2,18},{3,19},{4,20},{5,21},{6,22},{7,23},{8,24},{9,... | collective-permute-start | bytes 589832 | tf_op jit(solution)/shard_map/ppermute | solution.py:57
  38.5 9.1 %collective-permute-start.1 = (bf16[192,512]{1,0:T(8,128)(2,1)S(1)}, bf16[192,512]{1,0:T(8,128)(2,1)S(1)}, u32[]{:S(2)}, u32[]{:S(2)}) collective-permute-start(bf16[192,512]{1,0:T(8,128)(2,1)S(1)} %collective-permute-done.s0_ref), channel_id=1, source_target_pairs={{0,8},{1,9},{2,10},{3,11},{4,12},{5,13},{6,14},{7,15},{8,0},{9,1},... | collective-permute-start | bytes 589832 | tf_op jit(solution)/shard_map/ppermute | solution.py:57
  48.6 46.6 %collective-permute-start.4 = (bf16[768,512]{1,0:T(8,128)(2,1)}, bf16[768,512]{1,0:T(8,128)(2,1)S(1)}, u32[]{:S(2)}, u32[]{:S(2)}) collective-permute-start(bf16[768,512]{1,0:T(8,128)(2,1)} %pad_maximum_fusion), channel_id=1, source_target_pairs={{0,64},{1,65},{2,66},{3,67},{4,68},{5,69},{6,70},{7,71},{8,72},{9,... | collective-permute-start | bytes 2359304 | tf_op jit(solution)/shard_map/ppermute | solution.py:57
  76.8 11.1 %all-to-all-start.2 = ((f32[4,128,256]{2,1,0:T(8,128)}), f32[4,128,256]{2,1,0:T(8,128)S(1)}, u32[]{:S(2)}, u32[]{:S(2)}) async-start(f32[4,128,256]{2,1,0:T(8,128)} %broadcast_in_dim.30), calls=%async_computation.2 | async-start | bytes 1048576 | tf_op jit(solution)/shard_map/all_to_all | solution.py:34
  89.0 8.0 %all-to-all-start.3 = ((f32[2,512,256]{2,1,0:T(8,128)}), f32[2,512,256]{2,1,0:T(8,128)S(1)}, u32[]{:S(2)}, u32[]{:S(2)}) async-start(f32[2,512,256]{2,1,0:T(8,128)} %broadcast_in_dim.32), calls=%async_computation.3 | async-start | bytes 2097152 | tf_op jit(solution)/shard_map/all_to_all | solution.py:34
  107.6 29.2 %all-to-all-start.4 = ((bf16[64,40,128]{2,1,0:T(8,128)(2,1)}), bf16[64,40,128]{2,1,0:T(8,128)(2,1)S(1)}, u32[]{:S(2)}, u32[]{:S(2)}) async-start(bf16[64,40,128]{2,1,0:T(8,128)(2,1)} %get-tuple-element.10), calls=%async_computation.4 | async-start | bytes 1310720 | tf_op jit(solution)/shard_map/all_to_all | solution.py:34
  116.4 30.9 %collective-permute-start.5 = (bf16[192,512]{1,0:T(8,128)(2,1)S(1)}, bf16[192,512]{1,0:T(8,128)(2,1)S(1)}, u32[]{:S(2)}, u32[]{:S(2)}) collective-permute-start(bf16[192,512]{1,0:T(8,128)(2,1)S(1)} %get-tuple-element.12), channel_id=1, source_target_pairs={{0,0},{1,1},{2,2},{3,3},{4,4},{5,5},{6,6},{7,7},{8,128},{9,129},{1... | collective-permute-start | bytes 589832 | tf_op jit(solution)/shard_map/ppermute | solution.py:57
  148.7 5.4 %all-to-all-start.5 = ((bf16[2,8,8,2048]{3,2,1,0:T(8,128)(2,1)}), bf16[2,8,8,2048]{3,2,1,0:T(8,128)(2,1)S(1)}, u32[]{:S(2)}, u32[]{:S(2)}) async-start(bf16[2,8,8,2048]{3,2,1,0:T(8,128)(2,1)} %broadcast_in_dim.33), calls=%async_computation.5 | async-start | bytes 1048576 | tf_op jit(solution)/shard_map/all_to_all | solution.py:34

commit v6 on v5

--- a/solution.py
+++ b/solution.py
@@ -20,6 +20,7 @@
 HALF = BLOCK // 2
 SHARE = 3 * ROWS
 MESSAGE = 40
+DEEP = 4 * ROWS + 2 * SHARE
 WIDE = BLOCK // LANES
 
 stat_decay = 0.9
@@ -59,14 +60,6 @@
 
 def turned(shard):
     return moved(shard, lambda zl, co, zh, x, y: (x, co, zh, zl, y))
-
-
-def along_x(shard, flip):
-    return moved(shard, lambda zl, co, zh, x, y: (zl, co, zh, x ^ flip, y))
-
-
-def other_core(shard):
-    return moved(shard, lambda zl, co, zh, x, y: (zl, 1 - co, zh, x, y))
 
 
 def spread(shard, axis):
@@ -99,9 +92,20 @@
                 out_ref[i % 4 * 2 + w // 2, at : at + N, lanes] = rows.astype(BF16)
 
 
+def ring_kernel(mean_ref, share_ref, out_ref):
+    mean = mean_ref[...]
+    high = mean.astype(BF16)
+    low = (mean - high.astype(F32)).astype(BF16)
+    for k in range(SIZES[3]):
+        out_ref[k, 0 : 2 * ROWS, :] = high
+        out_ref[k, 2 * ROWS : 4 * ROWS, :] = low
+        for half in range(2):
+            rows = slice(4 * ROWS + half * SHARE, 4 * ROWS + (half + 1) * SHARE)
+            out_ref[k, rows, :] = share_ref[:, half * HALF : (half + 1) * HALF]
+
+
 def block_kernel(
-    own_ref, got_ref, s0_ref, s1_ref, s2_ref, s3_ref, twin_ref,
-    msg_ref, ret_ref, m_f, m_b, v_b, w_f, w_b, y_f, y_b, z_b, base_f,
+    own_ref, got_ref, msg_ref, ret_ref, m_f, m_b, v_b, w_f, w_b, y_f, y_b, z_b, base_f,
 ):
     own = pl.multiple_of(own_ref[0] * ROWS, ROWS)
     x = own_ref[0] >> 1
@@ -113,28 +117,29 @@
         cols = slice(half * HALF, (half + 1) * HALF)
         for k in range(4):
             for zh in range(2):
-                at = (k * 2 + zh) * ROWS
-                part = got_ref[half, at : at + ROWS, :]
+                at = zh * ROWS
+                high = got_ref[half, k, at : at + ROWS, :]
+                low = got_ref[half, k, 2 * ROWS + at : 3 * ROWS + at, :]
+                part = high.astype(F32) + low.astype(F32)
                 norm_g += jnp.sum(part * part, keepdims=True)
                 rows = slice((zh * 4 + k) * ROWS, (zh * 4 + k + 1) * ROWS)
                 y_f[rows, cols] = part
                 y_b[rows, cols] = part.astype(BF16)
-    shares = []
-    for flip, ref in enumerate((s0_ref, s1_ref, s2_ref, s3_ref)):
-        shares.append((pl.multiple_of((own_ref[0] ^ (2 * flip)) * ROWS, ROWS), ref, 0))
-        shares.append((pl.multiple_of((own_ref[0] ^ (2 * flip + 1)) * ROWS, ROWS), twin_ref, flip * SHARE))
     scale = jnp.ones((1, 1), F32)
     for side in range(2):
         w_f[side] = dot(y_b[...], y_b[...], (((1,), (1,)), ((0,), (0,)))[side])
         rows = w_f[side, pl.ds(own, ROWS), :]
         ret_ref[(1 + side) * ROWS : (2 + side) * ROWS, :] = rows.astype(BF16)
         total = jnp.zeros((1, 1), F32)
-        for at, ref, start in shares:
-            rows = pl.ds(at, ROWS)
-            old = ref[start + side * ROWS : start + (side + 1) * ROWS, :].astype(F32)
-            new = stat_decay * old + (1.0 - stat_decay) * w_f[side, rows, :]
-            m_f[side, rows, :] = new
-            total += jnp.sum(new * new, keepdims=True)
+        for k in range(N):
+            rows = slice(k * ROWS, (k + 1) * ROWS)
+            for half in range(2):
+                cols = slice(half * HALF, (half + 1) * HALF)
+                at = 4 * ROWS + half * SHARE + side * ROWS
+                old = got_ref[k % 2, k // 2, at : at + ROWS, :].astype(F32)
+                new = stat_decay * old + (1.0 - stat_decay) * w_f[side, rows, cols]
+                m_f[side, rows, cols] = new
+                total += jnp.sum(new * new, keepdims=True)
         frob = jnp.sqrt(total)
         scale = scale / jnp.sqrt(jnp.sqrt(frob))
         inverse = 1.0 / frob
@@ -142,8 +147,11 @@
             new = m_f[side, rows, :] * inverse
             m_f[side, rows, :] = new
             m_b[side, rows, :] = new.astype(BF16)
-    for at, ref, start in shares:
-        base_f[pl.ds(at, ROWS), :] = ref[start + 2 * ROWS : start + 3 * ROWS, :].astype(F32)
+    for k in range(N):
+        for half in range(2):
+            at = 4 * ROWS + half * SHARE + 2 * ROWS
+            cols = slice(half * HALF, (half + 1) * HALF)
+            base_f[k * ROWS : (k + 1) * ROWS, cols] = got_ref[k % 2, k // 2, at : at + ROWS, :].astype(F32)
 
     def apply_factors():
         for rows in spans:
@@ -260,16 +268,17 @@
     base = master[0] - (step_size * moment_decay) * momentum[0]
     share = jnp.concatenate([a.astype(BF16) for a in (left_stat[0], right_stat[0], base)], axis=0)
     s0 = turned(share)
-    shares = [s0] + [along_x(s0, flip) for flip in (1, 2, 3)]
-    twin = other_core(jnp.concatenate(shares, axis=0))
     (pieces,) = call(
         pack_kernel, [((N, 2 * ROWS, HALF), BF16)], [scratch(4, ROWS, LANES, dtype=F32)], mib=8
     )(gradients[0])
     pieces = exchanged(pieces, REP)
     mean = jnp.sum(pieces.astype(F32), axis=0) * (1.0 / N)
     mean = exchanged(mean.reshape(2 * N, N, HALF), PLANE)
-    mean = spread(mean.reshape(2 * ROWS, HALF), "x")
-    mean = spread(mean.reshape(BLOCK, HALF), "co")
+    (message,) = call(ring_kernel, [((SIZES[3], DEEP, HALF), BF16)], [], arrays=2, mib=8)(
+        mean.reshape(2 * ROWS, HALF), s0
+    )
+    message = exchanged(message, "x")
+    both = spread(message, "co")
     update = call(
         block_kernel,
         [((8 * N, MESSAGE, LANES), BF16), ((SHARE, BLOCK), BF16)],
@@ -286,11 +295,11 @@
         ],
         flops=56 * BLOCK**3,
         scalars=1,
-        arrays=6,
     )
-    messages, ret = update(own, mean, *shares, twin)
+    messages, ret = update(own, both)
+    got = exchanged(messages, SOLID)
+    ret, got = lax.optimization_barrier((ret, got))
     ret = turned(ret)
-    got = exchanged(messages, SOLID)
     half, graft = call(
         weight_kernel,
         [((N, N, N * HALF), BF16), ((N, LANES), F32)],

time: 156 us -> 147 us (0.942)
  the two profiles are of different devices: /device:TPU:27 before, /device:TPU:11 now
where the time goes in v6:
time: 147 us; the launch traced here: 146 us
  waiting for transfers between devices  49.6 us (34%)
  blocking collectives  45.4 us (31%)
  starting transfers between devices  31.4 us (21%)
  Pallas kernels  13 us (9%)
  other arithmetic  4.05 us (3%)
  local copies, waits for them, and re-layouts  1.78 us (1%)
    all_to_all x3, blocking collectives, exchanged(): return lax.all_to_all(pieces, axis, split_axis=0, concat_axis=0, tiled=True)  45.4 us
    all_to_all x3, waiting for transfers between devices, exchanged(): return lax.all_to_all(pieces, axis, split_axis=0, concat_axis=0, tiled=True)  27.2 us
    all_to_all x3, starting transfers between devices, exchanged(): return lax.all_to_all(pieces, axis, split_axis=0, concat_axis=0, tiled=True)  24.2 us
    ppermute x2, waiting for transfers between devices, moved(): return lax.ppermute(shard, ALL, pairs)  22.4 us
    pallas_call x1, Pallas kernels, step(): messages, ret = update(own, both)  9.61 us
    ppermute x2, starting transfers between devices, moved(): return lax.ppermute(shard, ALL, pairs)  7.17 us
  transfers between devices with their start and end apart: 5, of which 4 were waited for; matrix products, arithmetic and copies ran while one was open for 1% of the time, Pallas kernels for 1%

profile of v6, /device:TPU:11, one launch (start us, length us, event | category | flops | bytes accessed | tf_op | source)
XLA Modules:
  0.0 146.0 jit_solution(2412323405655735864)
XLA Ops:
  0.6 0.0 copy-start
  0.6 1.0 copy-done
  1.7 1.1 shard_map.84
  2.7 7.9 %all-to-all-start = ((bf16[8,128,256]{2,1,0:T(8,128)(2,1)}), bf16[8,128,256]{2,1,0:T(8,128)(2,1)S(1)}, u32[]{:S(2)}, u32[]{:S(2)}) async-start(bf16[8,128,256]{2,1,0:T(8,128)(2,1)} %shard_map.84), calls=%async_computation | async-start | bytes 1048576 | tf_op jit(solution)/shard_map/all_to_all | solution.py:35
  10.7 0.9 convert_bitcast_fusion.1
  11.6 1.1 fusion.3
  12.7 12.4 %all-to-all-done = bf16[8,128,256]{2,1,0:T(8,128)(2,1)S(1)} async-done(((bf16[8,128,256]{2,1,0:T(8,128)(2,1)}), bf16[8,128,256]{2,1,0:T(8,128)(2,1)S(1)}, u32[]{:S(2)}, u32[]{:S(2)}) %all-to-all-start) | async-done | bytes 524320 | tf_op jit(solution)/shard_map/all_to_all | solution.py:35
  25.0 0.1 convert_reduce_fusion
  25.1 0.7 multiply_bitcast_fusion
  25.8 12.7 %all-to-all-start.1 = ((f32[16,8,256]{2,1,0:T(8,128)}), f32[16,8,256]{2,1,0:T(8,128)S(1)}, u32[]{:S(2)}, u32[]{:S(2)}) async-start(f32[16,8,256]{2,1,0:T(8,128)} %multiply_bitcast_fusion), calls=%async_computation.1 | async-start | bytes 262144 | tf_op jit(solution)/shard_map/all_to_all | solution.py:35
  38.5 1.9 %collective-permute-start = (bf16[192,512]{1,0:T(8,128)(2,1)S(1)}, bf16[192,512]{1,0:T(8,128)(2,1)S(1)}, u32[]{:S(2)}, u32[]{:S(2)}) collective-permute-start(bf16[192,512]{1,0:T(8,128)(2,1)S(1)} %pad_maximum_fusion), channel_id=1, source_target_pairs={{0,0},{1,1},{2,2},{3,3},{4,4},{5,5},{6,6},{7,7},{8,128},{9,129},{1... | collective-permute-start | bytes 589832 | tf_op jit(solution)/shard_map/ppermute | solution.py:58
  40.5 16.0 %collective-permute-done.share_ref = bf16[192,512]{1,0:T(8,128)(2,1)S(1)} collective-permute-done((bf16[192,512]{1,0:T(8,128)(2,1)S(1)}, bf16[192,512]{1,0:T(8,128)(2,1)S(1)}, u32[]{:S(2)}, u32[]{:S(2)}) %collective-permute-start) | collective-permute-done | bytes 196640 | tf_op jit(solution)/shard_map/ppermute | solution.py:58
  56.5 0.0 all-to-all-done.1
  56.5 1.2 shard_map.85
  57.6 3.5 %all-to-all-start.2 = ((bf16[4,640,256]{2,1,0:T(8,128)(2,1)}), bf16[4,640,256]{2,1,0:T(8,128)(2,1)S(1)}, u32[]{:S(2)}, u32[]{:S(2)}) async-start(bf16[4,640,256]{2,1,0:T(8,128)(2,1)} %shard_map.85), calls=%async_computation.2 | async-start | bytes 2621440 | tf_op jit(solution)/shard_map/all_to_all | solution.py:35
  61.2 14.8 %all-to-all-done.2 = bf16[4,640,256]{2,1,0:T(8,128)(2,1)S(1)} async-done(((bf16[4,640,256]{2,1,0:T(8,128)(2,1)}), bf16[4,640,256]{2,1,0:T(8,128)(2,1)S(1)}, u32[]{:S(2)}, u32[]{:S(2)}) %all-to-all-start.2) | async-done | bytes 1310752 | tf_op jit(solution)/shard_map/all_to_all | solution.py:35
  76.0 0.2 broadcast_in_dim.10
  76.1 7.9 %all_to_all.30.got_ref = bf16[2,4,640,256]{3,2,1,0:T(8,128)(2,1)S(1)} all-to-all(bf16[2,4,640,256]{3,2,1,0:T(8,128)(2,1)S(1)} %broadcast_in_dim.10), channel_id=1, replica_groups=mesh['zl'=4,'co'=2,'zh'=2,'x'=4,'y'=8] {'co'}, dimensions={0} | all-to-all | bytes 5242880 | tf_op jit(solution)/shard_map/all_to_all | solution.py:35
  84.0 9.6 %shard_map.86 = (bf16[64,40,128]{2,1,0:T(8,128)(2,1)S(1)}, bf16[192,512]{1,0:T(8,128)(2,1)S(1)}) custom-call(s32[1]{0:T(128)} %bitcast.own_ref, bf16[2,4,640,256]{3,2,1,0:T(8,128)(2,1)S(1)} %all_to_all.30.got_ref), custom_call_target="tpu_custom_call" | custom-call | flops 7516192768 | bytes 1048576 | tf_op jit(solution)/shard_map/pallas_call | solution.py:299
  93.7 0.0 copy-start.1
  93.7 0.0 copy-start.2
  93.7 0.0 copy-start.3
  93.7 31.4 %all_to_all.31.got_ref = bf16[64,40,128]{2,1,0:T(8,128)(2,1)S(1)} all-to-all(bf16[64,40,128]{2,1,0:T(8,128)(2,1)S(1)} %get-tuple-element.13), channel_id=1, replica_groups=mesh['zl'=4,'co'=2,'zh'=2,'x'=4,'y'=8] {'zl','zh','y'}, dimensions={0} | all-to-all | bytes 1310720 | tf_op jit(solution)/shard_map/all_to_all | solution.py:35
  125.1 5.2 %collective-permute-start.1 = (bf16[192,512]{1,0:T(8,128)(2,1)S(1)}, bf16[192,512]{1,0:T(8,128)(2,1)S(1)}, u32[]{:S(2)}, u32[]{:S(2)}) collective-permute-start(bf16[192,512]{1,0:T(8,128)(2,1)S(1)} %get-tuple-element.16), channel_id=1, source_target_pairs={{0,0},{1,1},{2,2},{3,3},{4,4},{5,5},{6,6},{7,7},{8,128},{9,129},{1... | collective-permute-start | bytes 589832 | tf_op jit(solution)/shard_map/ppermute | solution.py:58
  130.4 0.4 shard_map.87
  130.8 6.1 %all_to_all.32.got_ref = bf16[2,8,8,2048]{3,2,1,0:T(8,128)(2,1)S(1)} all-to-all(bf16[2,8,8,2048]{3,2,1,0:T(8,128)(2,1)S(1)} %broadcast_in_dim.22), channel_id=1, replica_groups=mesh['zl'=4,'co'=2,'zh'=2,'x'=4,'y'=8] {'co'}, dimensions={0} | all-to-all | bytes 1048576 | tf_op jit(solution)/shard_map/all_to_all | solution.py:35
  136.9 0.8 shard_map.88
  137.7 6.4 %collective-permute-done.1 = bf16[192,512]{1,0:T(8,128)(2,1)S(1)} collective-permute-done((bf16[192,512]{1,0:T(8,128)(2,1)S(1)}, bf16[192,512]{1,0:T(8,128)(2,1)S(1)}, u32[]{:S(2)}, u32[]{:S(2)}) %collective-permute-start.1) | collective-permute-done | bytes 196640 | tf_op jit(solution)/shard_map/ppermute | solution.py:58
  144.2 0.5 slice.12
  144.7 0.0 copy-done.1
  144.7 0.0 copy-done.2
  144.7 0.0 copy-done.3
  144.7 1.3 fusion
  (2 shorter events, 0.1 us)
Async XLA Ops:
  0.6 1.0 copy-start
  2.7 22.3 %all-to-all-start = ((bf16[8,128,256]{2,1,0:T(8,128)(2,1)}), bf16[8,128,256]{2,1,0:T(8,128)(2,1)S(1)}, u32[]{:S(2)}, u32[]{:S(2)}) async-start(bf16[8,128,256]{2,1,0:T(8,128)(2,1)} %shard_map.84), calls=%async_computation | async-start | bytes 1048576 | tf_op jit(solution)/shard_map/all_to_all | solution.py:35
  25.8 30.7 %all-to-all-start.1 = ((f32[16,8,256]{2,1,0:T(8,128)}), f32[16,8,256]{2,1,0:T(8,128)S(1)}, u32[]{:S(2)}, u32[]{:S(2)}) async-start(f32[16,8,256]{2,1,0:T(8,128)} %multiply_bitcast_fusion), calls=%async_computation.1 | async-start | bytes 262144 | tf_op jit(solution)/shard_map/all_to_all | solution.py:35
  38.5 17.9 %collective-permute-start = (bf16[192,512]{1,0:T(8,128)(2,1)S(1)}, bf16[192,512]{1,0:T(8,128)(2,1)S(1)}, u32[]{:S(2)}, u32[]{:S(2)}) collective-permute-start(bf16[192,512]{1,0:T(8,128)(2,1)S(1)} %pad_maximum_fusion), channel_id=1, source_target_pairs={{0,0},{1,1},{2,2},{3,3},{4,4},{5,5},{6,6},{7,7},{8,128},{9,129},{1... | collective-permute-start | bytes 589832 | tf_op jit(solution)/shard_map/ppermute | solution.py:58
  57.6 18.3 %all-to-all-start.2 = ((bf16[4,640,256]{2,1,0:T(8,128)(2,1)}), bf16[4,640,256]{2,1,0:T(8,128)(2,1)S(1)}, u32[]{:S(2)}, u32[]{:S(2)}) async-start(bf16[4,640,256]{2,1,0:T(8,128)(2,1)} %shard_map.85), calls=%async_computation.2 | async-start | bytes 2621440 | tf_op jit(solution)/shard_map/all_to_all | solution.py:35
  93.7 51.0 %copy-start.1 = (f32[1,64,512]{2,1,0:T(8,128)S(1)}, f32[1,64,512]{2,1,0:T(8,128)}, u32[]{:S(2)}) copy-start(f32[1,64,512]{2,1,0:T(8,128)} %param.6) | copy-start | bytes 393220
  93.7 51.0 %copy-start.2 = (f32[1,64,512]{2,1,0:T(8,128)S(1)}, f32[1,64,512]{2,1,0:T(8,128)}, u32[]{:S(2)}) copy-start(f32[1,64,512]{2,1,0:T(8,128)} %param.8) | copy-start | bytes 393220
  93.7 51.0 %copy-start.3 = (f32[1,64,512]{2,1,0:T(8,128)S(1)}, f32[1,64,512]{2,1,0:T(8,128)}, u32[]{:S(2)}) copy-start(f32[1,64,512]{2,1,0:T(8,128)} %param.7) | copy-start | bytes 393220
  125.1 19.0 %collective-permute-start.1 = (bf16[192,512]{1,0:T(8,128)(2,1)S(1)}, bf16[192,512]{1,0:T(8,128)(2,1)S(1)}, u32[]{:S(2)}, u32[]{:S(2)}) collective-permute-start(bf16[192,512]{1,0:T(8,128)(2,1)S(1)} %get-tuple-element.16), channel_id=1, source_target_pairs={{0,0},{1,1},{2,2},{3,3},{4,4},{5,5},{6,6},{7,7},{8,128},{9,129},{1... | collective-permute-start | bytes 589832 | tf_op jit(solution)/shard_map/ppermute | solution.py:58
